TPU v7x, 32 devices: a whole 2x2x4 slice. The times are simulated.
32 devices in a mesh: tp: 4 (over z), cp: 8 (over y, x, core).
Axes of the slice: x: 2, y: 2, z: 4, core: 2. Of those that a mesh axis runs over, the one named last changes fastest.
Arguments:
- hidden: bfloat16 [8, 1024, 4096], P(None, 'cp')
- grad_out: bfloat16 [8, 1024, 4096], P(None, 'cp')
- w_query: bfloat16 [4096, 32, 128], P(None, 'tp')
- w_key: bfloat16 [4096, 128], replicated
- w_value: bfloat16 [4096, 128], replicated
- w_out: bfloat16 [32, 128, 4096], P('tp')
Outputs:
- output 1: bfloat16 [8, 1024, 4096], P(None, 'cp')
- output 2: bfloat16 [8, 1024, 4096], P(None, 'cp')
- output 3: float32 [4096, 32, 128], P(None, 'tp')
- output 4: float32 [4096, 128], replicated
- output 5: float32 [4096, 128], replicated
- output 6: float32 [32, 128, 4096], P('tp')
All inputs are finite; a program needn't handle non-finite values.
Results may differ from a plain program's by a relative error of at most 0.0110117.
Values are sent between devices in bfloat16 or wider.
A program may use at most 1 GiB of HBM per device.

v0:
```python
import jax
import jax.numpy as jnp
from jax import lax
from jax.sharding import PartitionSpec as P

ROPE_BASE = 10000.0


def rope_tables(positions, head_dim):
    half_dim = head_dim // 2
    inv_freq = 1.0 / jnp.power(ROPE_BASE, jnp.arange(half_dim, dtype=jnp.float32) * (2.0 / head_dim))
    angles = positions.astype(jnp.float32)[:, None] * inv_freq[None, :]
    return jnp.cos(angles), jnp.sin(angles)


def rotate(rot_in, cos_tab, sin_tab):
    half_dim = rot_in.shape[-1] // 2
    low_half = rot_in[..., :half_dim]
    high_half = rot_in[..., half_dim:]
    return jnp.concatenate([low_half * cos_tab - high_half * sin_tab, high_half * cos_tab + low_half * sin_tab], axis=-1)


def unrotate(rot_in, cos_tab, sin_tab):
    half_dim = rot_in.shape[-1] // 2
    low_half = rot_in[..., :half_dim]
    high_half = rot_in[..., half_dim:]
    return jnp.concatenate([low_half * cos_tab + high_half * sin_tab, high_half * cos_tab - low_half * sin_tab], axis=-1)


def pair_scores(queries, key_blk, q_start, k_start):
    scores = jnp.einsum("bhqe,bke->bhqk", queries, key_blk, preferred_element_type=jnp.float32)
    q_pos = q_start + jnp.arange(queries.shape[2])
    k_pos = k_start + jnp.arange(key_blk.shape[1])
    allowed = k_pos[None, :] <= q_pos[:, None]
    return jnp.where(allowed, scores, -jnp.inf)


def forward_update(queries, kv_blk, q_start, k_start, soft_stats):
    run_max, run_sum, run_acc = soft_stats
    scores = pair_scores(queries, kv_blk[:, 0], q_start, k_start)
    new_max = jnp.maximum(run_max, jnp.max(scores, axis=-1))
    rescale = jnp.exp(run_max - new_max)
    weights = jnp.exp(scores - new_max[..., None])
    new_sum = run_sum * rescale + jnp.sum(weights, axis=-1)
    new_acc = run_acc * rescale[..., None] + jnp.einsum("bhqk,bke->bhqe", weights.astype(jnp.bfloat16), kv_blk[:, 1], preferred_element_type=jnp.float32)
    return new_max, new_sum, new_acc


def backward_update(queries, d_out, row_lse, row_delta, kv_blk, q_start, k_start):
    scores = pair_scores(queries, kv_blk[:, 0], q_start, k_start)
    prob_blk = jnp.exp(scores - row_lse[..., None])
    d_prob = jnp.einsum("bhqe,bke->bhqk", d_out, kv_blk[:, 1], preferred_element_type=jnp.float32)
    d_score = (prob_blk * (d_prob - row_delta[..., None])).astype(jnp.bfloat16)
    dq_part = jnp.einsum("bhqk,bke->bhqe", d_score, kv_blk[:, 0], preferred_element_type=jnp.float32)
    dk_part = jnp.einsum("bhqk,bhqe->bke", d_score, queries, preferred_element_type=jnp.float32)
    dv_part = jnp.einsum("bhqk,bhqe->bke", prob_blk.astype(jnp.bfloat16), d_out, preferred_element_type=jnp.float32)
    return dq_part, jnp.stack([dk_part, dv_part], axis=1)


def solution(mesh):
    cp_size = mesh.shape["cp"]
    shift_pairs = [(src_idx, (src_idx + 1) % cp_size) for src_idx in range(cp_size)]

    def local_program(hidden, grad_out, w_query, w_key, w_value, w_out):
        n_batch, block_len = hidden.shape[0], hidden.shape[1]
        n_local = w_query.shape[1]
        head_dim = w_key.shape[1]
        q_scale = head_dim ** -0.5
        cp_idx = lax.axis_index("cp")
        q_start = cp_idx * block_len
        cos_tab, sin_tab = rope_tables(q_start + jnp.arange(block_len), head_dim)
        q_pre = jnp.einsum("bsd,dhe->bhse", hidden, w_query, preferred_element_type=jnp.float32)
        queries = (rotate(q_pre, cos_tab, sin_tab) * q_scale).astype(jnp.bfloat16)
        key_pre = jnp.einsum("bsd,de->bse", hidden, w_key, preferred_element_type=jnp.float32)
        key_loc = rotate(key_pre, cos_tab, sin_tab).astype(jnp.bfloat16)
        val_loc = jnp.einsum("bsd,de->bse", hidden, w_value, preferred_element_type=jnp.float32).astype(jnp.bfloat16)
        kv_loc = jnp.stack([key_loc, val_loc], axis=1)

        def fwd_compute(step_idx, kv_blk, soft_stats):
            k_start = ((cp_idx - step_idx) % cp_size) * block_len
            return lax.cond(step_idx <= cp_idx, lambda stats_in: forward_update(queries, kv_blk, q_start, k_start, stats_in), lambda stats_in: stats_in, soft_stats)

        def fwd_body(step_idx, loop_state):
            kv_blk, soft_stats = loop_state
            soft_stats = fwd_compute(step_idx, kv_blk, soft_stats)
            return lax.ppermute(kv_blk, "cp", shift_pairs), soft_stats

        stats_init = (jnp.full((n_batch, n_local, block_len), -jnp.inf, jnp.float32), jnp.zeros((n_batch, n_local, block_len), jnp.float32), jnp.zeros((n_batch, n_local, block_len, head_dim), jnp.float32))
        kv_blk, soft_stats = lax.fori_loop(0, cp_size - 1, fwd_body, (kv_loc, stats_init))
        run_max, run_sum, run_acc = fwd_compute(cp_size - 1, kv_blk, soft_stats)
        attn_heads = (run_acc / run_sum[..., None]).astype(jnp.bfloat16)
        row_lse = run_max + jnp.log(run_sum)
        out_part = jnp.einsum("cirf,ife->cre", attn_heads, w_out, preferred_element_type=jnp.float32)
        attn_out = lax.psum(out_part, "tp").astype(jnp.bfloat16)
        d_out = jnp.einsum("cre,ife->cirf", grad_out, w_out, preferred_element_type=jnp.float32).astype(jnp.bfloat16)
        row_delta = jnp.einsum("bhqe,bhqe->bhq", d_out, attn_heads, preferred_element_type=jnp.float32)

        def bwd_compute(step_idx, kv_blk, dkv_blk, dq_acc):
            k_start = ((cp_idx - step_idx) % cp_size) * block_len

            def active(acc_pair):
                dq_in, dkv_in = acc_pair
                dq_part, dkv_part = backward_update(queries, d_out, row_lse, row_delta, kv_blk, q_start, k_start)
                return dq_in + dq_part, dkv_in + dkv_part

            return lax.cond(step_idx <= cp_idx, active, lambda acc_pair: acc_pair, (dq_acc, dkv_blk))

        def bwd_body(step_idx, loop_state):
            kv_blk, dkv_blk, dq_acc = loop_state
            dq_acc, dkv_blk = bwd_compute(step_idx, kv_blk, dkv_blk, dq_acc)
            kv_blk = lax.ppermute(kv_blk, "cp", shift_pairs)
            dkv_blk = lax.ppermute(dkv_blk, "cp", shift_pairs)
            return kv_blk, dkv_blk, dq_acc

        dkv_init = jnp.zeros((n_batch, 2, block_len, head_dim), jnp.float32)
        dq_init = jnp.zeros((n_batch, n_local, block_len, head_dim), jnp.float32)
        kv_blk, dkv_blk, dq_acc = lax.fori_loop(0, cp_size - 1, bwd_body, (kv_loc, dkv_init, dq_init))
        dq_acc, dkv_blk = bwd_compute(cp_size - 1, kv_blk, dkv_blk, dq_acc)
        dkv_blk = lax.ppermute(dkv_blk, "cp", shift_pairs)
        dkv_full = lax.psum(dkv_blk, "tp")
        dq_pre = (unrotate(dq_acc, cos_tab, sin_tab) * q_scale).astype(jnp.bfloat16)
        dk_pre = unrotate(dkv_full[:, 0], cos_tab, sin_tab).astype(jnp.bfloat16)
        dv_pre = dkv_full[:, 1].astype(jnp.bfloat16)
        d_w_query = lax.psum(jnp.einsum("cre,cirf->eif", hidden, dq_pre, preferred_element_type=jnp.float32), "cp")
        d_w_out = lax.psum(jnp.einsum("cirf,cre->ife", attn_heads, grad_out, preferred_element_type=jnp.float32), "cp")
        d_w_key = lax.psum(jnp.einsum("cre,crf->ef", hidden, dk_pre, preferred_element_type=jnp.float32), "cp")
        d_w_value = lax.psum(jnp.einsum("cre,crf->ef", hidden, dv_pre, preferred_element_type=jnp.float32), "cp")
        dh_heads = lax.psum(jnp.einsum("cirf,eif->cre", dq_pre, w_query, preferred_element_type=jnp.float32), "tp")
        dh_kv = jnp.einsum("crf,ef->cre", dk_pre, w_key, preferred_element_type=jnp.float32) + jnp.einsum("crf,ef->cre", dv_pre, w_value, preferred_element_type=jnp.float32)
        d_hidden = (dh_heads + dh_kv).astype(jnp.bfloat16)
        return attn_out, d_hidden, d_w_query, d_w_key, d_w_value, d_w_out

    row_spec = P(None, "cp", None)
    return jax.shard_map(local_program, mesh=mesh, in_specs=(row_spec, row_spec, P(None, "tp", None), P(), P(), P("tp", None, None)), out_specs=(row_spec, row_spec, P(None, "tp", None), P(), P(), P("tp", None, None)), check_vma=False)
```

profile of v0, /device:TPU:0, one launch (start us, length us, event | category | flops | bytes accessed | tf_op | source)
XLA Modules:
  0.0 1692.4 jit_solution(16051617830282234261)
XLA Ops:
  7.3 13.8 convert_bitcast_fusion
  42.8 27.1 %fusion.81 = f32[8,8,128,128]{2,3,0,1:T(8,128)S(1)} fusion(bf16[8,128,4096]{2,1,0:T(8,128)(2,1)} %param.18, bf16[4096,8,128,1]{2,1,0,3:T(8,128)(2,1)} %bitcast.165), kind=kOutput, calls=%fused_computation.111 | convolution fusion | flops 8589934592 | bytes 20971520 | tf_op jit(solution)/shard_map/bsd,dhe->bhse/dot_general | solution.py:72
  77.9 80.5 %while.40 = (s32[]{:T(128)}, bf16[8,2,128,128]{3,2,0,1:T(8,128)(2,1)}, f32[8,8,128]{2,1,0:T(8,128)S(1)}, f32[8,8,128]{2,1,0:T(8,128)S(1)}, f32[8,8,128,128]{3,2,...) while((s32[]{:T(128)}, bf16[8,2,128,128]{3,2,0,1:T(8,128)(2,1)}, ...), condition=%wide.region_5.6_spmd, body=%wide.region_0.5_spmd.sunk | while | flops 547389696 | bytes 60885464 | solution.py:89
  126.1 9.5 collective-permute-done
  137.5 9.5 collective-permute-done
  167.1 250.9 %while.41 = (s32[]{:T(128)}, bf16[8,2,128,128]{3,2,0,1:T(8,128)(2,1)}, f32[8,2,128,128]{3,2,0,1:T(8,128)}, f32[8,8,128,128]{3,2,1,0:T(8,128)}, s32[]{:T(128)}, /...) while((s32[]{:T(128)}, ...), condition=%wide.region_14.15_spmd, body=%wide.region_11.14_spmd.sunk | while | flops 1352155392 | bytes 60705288 | solution.py:117
  169.0 15.0 conditional.9
  184.0 23.3 %collective-permute-done.2 = f32[8,2,128,128]{3,2,0,1:T(8,128)} collective-permute-done((f32[8,2,128,128]{3,2,0,1:T(8,128)}, f32[8,2,128,128]{3,2,0,1:T(8,128)}, u32[]{:S(2)}, u32[]{:S(2)}) %collective-permute-start.2) | collective-permute-done | bytes 1048608 | tf_op jit(solution)/shard_map/while/body/eval_jaxpr/ppermute | solution.py:112
  218.9 22.5 %collective-permute-done.2 = f32[8,2,128,128]{3,2,0,1:T(8,128)} collective-permute-done((f32[8,2,128,128]{3,2,0,1:T(8,128)}, f32[8,2,128,128]{3,2,0,1:T(8,128)}, u32[]{:S(2)}, u32[]{:S(2)}) %collective-permute-start.2) | collective-permute-done | bytes 1048608 | tf_op jit(solution)/shard_map/while/body/eval_jaxpr/ppermute | solution.py:112
  255.6 20.0 %collective-permute-done.2 = f32[8,2,128,128]{3,2,0,1:T(8,128)} collective-permute-done((f32[8,2,128,128]{3,2,0,1:T(8,128)}, f32[8,2,128,128]{3,2,0,1:T(8,128)}, u32[]{:S(2)}, u32[]{:S(2)}) %collective-permute-start.2) | collective-permute-done | bytes 1048608 | tf_op jit(solution)/shard_map/while/body/eval_jaxpr/ppermute | solution.py:112
  283.1 26.7 %collective-permute-done.2 = f32[8,2,128,128]{3,2,0,1:T(8,128)} collective-permute-done((f32[8,2,128,128]{3,2,0,1:T(8,128)}, f32[8,2,128,128]{3,2,0,1:T(8,128)}, u32[]{:S(2)}, u32[]{:S(2)}) %collective-permute-start.2) | collective-permute-done | bytes 1048608 | tf_op jit(solution)/shard_map/while/body/eval_jaxpr/ppermute | solution.py:112
  317.3 26.7 %collective-permute-done.2 = f32[8,2,128,128]{3,2,0,1:T(8,128)} collective-permute-done((f32[8,2,128,128]{3,2,0,1:T(8,128)}, f32[8,2,128,128]{3,2,0,1:T(8,128)}, u32[]{:S(2)}, u32[]{:S(2)}) %collective-permute-start.2) | collective-permute-done | bytes 1048608 | tf_op jit(solution)/shard_map/while/body/eval_jaxpr/ppermute | solution.py:112
  351.5 26.7 %collective-permute-done.2 = f32[8,2,128,128]{3,2,0,1:T(8,128)} collective-permute-done((f32[8,2,128,128]{3,2,0,1:T(8,128)}, f32[8,2,128,128]{3,2,0,1:T(8,128)}, u32[]{:S(2)}, u32[]{:S(2)}) %collective-permute-start.2) | collective-permute-done | bytes 1048608 | tf_op jit(solution)/shard_map/while/body/eval_jaxpr/ppermute | solution.py:112
  385.7 26.7 %collective-permute-done.2 = f32[8,2,128,128]{3,2,0,1:T(8,128)} collective-permute-done((f32[8,2,128,128]{3,2,0,1:T(8,128)}, f32[8,2,128,128]{3,2,0,1:T(8,128)}, u32[]{:S(2)}, u32[]{:S(2)}) %collective-permute-start.2) | collective-permute-done | bytes 1048608 | tf_op jit(solution)/shard_map/while/body/eval_jaxpr/ppermute | solution.py:112
  418.0 11.1 conditional.5
  434.5 16.2 convolution_bitcast_fusion.3
  457.7 13.9 convolution_bitcast_fusion.4
  471.6 14.7 convolution_bitcast_fusion.1
  486.4 13.8 convolution_bitcast_fusion.2
  500.2 557.0 %all-reduce.8.cloned.1.call-done = (f32[8,128,4096]{2,1,0:T(8,128)}, f32[8,2,128,128]{2,3,0,1:T(8,128)}) async-done(((f32[8,128,4096]{2,1,0:T(8,128)}, f32[8,2,128,128]{2,3,0,1:T(8,128)}), (f32[8,128,4096]{2,1,0:T(8,128)}, f32[8,2,128,128]{2,3,0,1:T(8,128)})) %all-reduce.8.cloned.1.call-update) | async-done | bytes 17825808 | tf_op jit(solution)/shard_map/psum | solution.py:128
  1070.5 556.9 %all-reduce.9 = bf16[8,128,4096]{2,1,0:T(8,128)(2,1)} all-reduce(f32[8,128,4096]{2,1,0:T(8,128)} %convolution_bitcast_fusion.4), channel_id=1, replica_groups=mesh['tp'=4,'cp'=8] {'tp'}, use_global_device_ids=true, to_apply=%region_10.11 | all-reduce | flops 4194304 | bytes 25165824 | tf_op jit(solution)/shard_map/psum | solution.py:94
  1635.9 15.4 add_convert_fusion
  1651.2 17.5 %copy.42 = f32[4096,8,128]{2,1,0:T(8,128)} copy(f32[4096,8,128]{0,2,1:T(8,128)} %get-tuple-element.947) | data formatting | bytes 33554432
  1673.5 11.7 copy.178
  (153 shorter events, 236.7 us)
Async XLA Ops:
  7.2 1050.0 %all-reduce.8.cloned.1.call-start = ((), (), s32[]{:S(2)}) async-start(), calls=%async_computation.1 | async-start | bytes 35651584 | tf_op jit(solution)/shard_map/psum | solution.py:128
  79.8 10.3 collective-permute-start
  92.0 9.5 collective-permute-start
  103.3 9.5 collective-permute-start
  114.7 9.5 collective-permute-start
  126.1 9.5 collective-permute-start
  137.5 9.5 collective-permute-start
  148.9 9.5 collective-permute-start
  184.0 23.3 %collective-permute-start.2 = (f32[8,2,128,128]{3,2,0,1:T(8,128)}, f32[8,2,128,128]{3,2,0,1:T(8,128)}, u32[]{:S(2)}, u32[]{:S(2)}) collective-permute-start(f32[8,2,128,128]{3,2,0,1:T(8,128)} %get-tuple-element.1103), channel_id=1, source_target_pairs={{0,1},{1,2},{2,3},{3,4},{4,5},{5,6},{6,7},{7,0},{8,9},{9,10},{10,1... | collective-permute-start | bytes 3145736 | tf_op jit(solution)/shard_map/while/body/eval_jaxpr/ppermute | solution.py:112
  184.0 28.9 %collective-permute-start.1 = (bf16[8,2,128,128]{3,2,0,1:T(8,128)(2,1)}, bf16[8,2,128,128]{3,2,0,1:T(8,128)(2,1)}, u32[]{:S(2)}, u32[]{:S(2)}) collective-permute-start(bf16[8,2,128,128]{3,2,0,1:T(8,128)(2,1)} %copy.156), channel_id=1, source_target_pairs={{0,1},{1,2},{2,3},{3,4},{4,5},{5,6},{6,7},{7,0},{8,9},{9,10},{10,1... | collective-permute-start | bytes 1572872 | tf_op jit(solution)/shard_map/while/body/eval_jaxpr/ppermute | solution.py:111
  214.7 26.7 %collective-permute-start.2 = (f32[8,2,128,128]{3,2,0,1:T(8,128)}, f32[8,2,128,128]{3,2,0,1:T(8,128)}, u32[]{:S(2)}, u32[]{:S(2)}) collective-permute-start(f32[8,2,128,128]{3,2,0,1:T(8,128)} %get-tuple-element.1103), channel_id=1, source_target_pairs={{0,1},{1,2},{2,3},{3,4},{4,5},{5,6},{6,7},{7,0},{8,9},{9,10},{10,1... | collective-permute-start | bytes 3145736 | tf_op jit(solution)/shard_map/while/body/eval_jaxpr/ppermute | solution.py:112
  216.4 30.6 %collective-permute-start.1 = (bf16[8,2,128,128]{3,2,0,1:T(8,128)(2,1)}, bf16[8,2,128,128]{3,2,0,1:T(8,128)(2,1)}, u32[]{:S(2)}, u32[]{:S(2)}) collective-permute-start(bf16[8,2,128,128]{3,2,0,1:T(8,128)(2,1)} %copy.156), channel_id=1, source_target_pairs={{0,1},{1,2},{2,3},{3,4},{4,5},{5,6},{6,7},{7,0},{8,9},{9,10},{10,1... | collective-permute-start | bytes 1572872 | tf_op jit(solution)/shard_map/while/body/eval_jaxpr/ppermute | solution.py:111
  248.9 26.7 %collective-permute-start.2 = (f32[8,2,128,128]{3,2,0,1:T(8,128)}, f32[8,2,128,128]{3,2,0,1:T(8,128)}, u32[]{:S(2)}, u32[]{:S(2)}) collective-permute-start(f32[8,2,128,128]{3,2,0,1:T(8,128)} %get-tuple-element.1103), channel_id=1, source_target_pairs={{0,1},{1,2},{2,3},{3,4},{4,5},{5,6},{6,7},{7,0},{8,9},{9,10},{10,1... | collective-permute-start | bytes 3145736 | tf_op jit(solution)/shard_map/while/body/eval_jaxpr/ppermute | solution.py:112
  248.9 32.3 %collective-permute-start.1 = (bf16[8,2,128,128]{3,2,0,1:T(8,128)(2,1)}, bf16[8,2,128,128]{3,2,0,1:T(8,128)(2,1)}, u32[]{:S(2)}, u32[]{:S(2)}) collective-permute-start(bf16[8,2,128,128]{3,2,0,1:T(8,128)(2,1)} %copy.156), channel_id=1, source_target_pairs={{0,1},{1,2},{2,3},{3,4},{4,5},{5,6},{6,7},{7,0},{8,9},{9,10},{10,1... | collective-permute-start | bytes 1572872 | tf_op jit(solution)/shard_map/while/body/eval_jaxpr/ppermute | solution.py:111
  283.1 26.7 %collective-permute-start.2 = (f32[8,2,128,128]{3,2,0,1:T(8,128)}, f32[8,2,128,128]{3,2,0,1:T(8,128)}, u32[]{:S(2)}, u32[]{:S(2)}) collective-permute-start(f32[8,2,128,128]{3,2,0,1:T(8,128)} %get-tuple-element.1103), channel_id=1, source_target_pairs={{0,1},{1,2},{2,3},{3,4},{4,5},{5,6},{6,7},{7,0},{8,9},{9,10},{10,1... | collective-permute-start | bytes 3145736 | tf_op jit(solution)/shard_map/while/body/eval_jaxpr/ppermute | solution.py:112
  283.1 32.3 %collective-permute-start.1 = (bf16[8,2,128,128]{3,2,0,1:T(8,128)(2,1)}, bf16[8,2,128,128]{3,2,0,1:T(8,128)(2,1)}, u32[]{:S(2)}, u32[]{:S(2)}) collective-permute-start(bf16[8,2,128,128]{3,2,0,1:T(8,128)(2,1)} %copy.156), channel_id=1, source_target_pairs={{0,1},{1,2},{2,3},{3,4},{4,5},{5,6},{6,7},{7,0},{8,9},{9,10},{10,1... | collective-permute-start | bytes 1572872 | tf_op jit(solution)/shard_map/while/body/eval_jaxpr/ppermute | solution.py:111
  317.3 26.7 %collective-permute-start.2 = (f32[8,2,128,128]{3,2,0,1:T(8,128)}, f32[8,2,128,128]{3,2,0,1:T(8,128)}, u32[]{:S(2)}, u32[]{:S(2)}) collective-permute-start(f32[8,2,128,128]{3,2,0,1:T(8,128)} %get-tuple-element.1103), channel_id=1, source_target_pairs={{0,1},{1,2},{2,3},{3,4},{4,5},{5,6},{6,7},{7,0},{8,9},{9,10},{10,1... | collective-permute-start | bytes 3145736 | tf_op jit(solution)/shard_map/while/body/eval_jaxpr/ppermute | solution.py:112
  317.3 32.3 %collective-permute-start.1 = (bf16[8,2,128,128]{3,2,0,1:T(8,128)(2,1)}, bf16[8,2,128,128]{3,2,0,1:T(8,128)(2,1)}, u32[]{:S(2)}, u32[]{:S(2)}) collective-permute-start(bf16[8,2,128,128]{3,2,0,1:T(8,128)(2,1)} %copy.156), channel_id=1, source_target_pairs={{0,1},{1,2},{2,3},{3,4},{4,5},{5,6},{6,7},{7,0},{8,9},{9,10},{10,1... | collective-permute-start | bytes 1572872 | tf_op jit(solution)/shard_map/while/body/eval_jaxpr/ppermute | solution.py:111
  351.5 26.7 %collective-permute-start.2 = (f32[8,2,128,128]{3,2,0,1:T(8,128)}, f32[8,2,128,128]{3,2,0,1:T(8,128)}, u32[]{:S(2)}, u32[]{:S(2)}) collective-permute-start(f32[8,2,128,128]{3,2,0,1:T(8,128)} %get-tuple-element.1103), channel_id=1, source_target_pairs={{0,1},{1,2},{2,3},{3,4},{4,5},{5,6},{6,7},{7,0},{8,9},{9,10},{10,1... | collective-permute-start | bytes 3145736 | tf_op jit(solution)/shard_map/while/body/eval_jaxpr/ppermute | solution.py:112
  351.5 32.3 %collective-permute-start.1 = (bf16[8,2,128,128]{3,2,0,1:T(8,128)(2,1)}, bf16[8,2,128,128]{3,2,0,1:T(8,128)(2,1)}, u32[]{:S(2)}, u32[]{:S(2)}) collective-permute-start(bf16[8,2,128,128]{3,2,0,1:T(8,128)(2,1)} %copy.156), channel_id=1, source_target_pairs={{0,1},{1,2},{2,3},{3,4},{4,5},{5,6},{6,7},{7,0},{8,9},{9,10},{10,1... | collective-permute-start | bytes 1572872 | tf_op jit(solution)/shard_map/while/body/eval_jaxpr/ppermute | solution.py:111
  385.7 26.7 %collective-permute-start.2 = (f32[8,2,128,128]{3,2,0,1:T(8,128)}, f32[8,2,128,128]{3,2,0,1:T(8,128)}, u32[]{:S(2)}, u32[]{:S(2)}) collective-permute-start(f32[8,2,128,128]{3,2,0,1:T(8,128)} %get-tuple-element.1103), channel_id=1, source_target_pairs={{0,1},{1,2},{2,3},{3,4},{4,5},{5,6},{6,7},{7,0},{8,9},{9,10},{10,1... | collective-permute-start | bytes 3145736 | tf_op jit(solution)/shard_map/while/body/eval_jaxpr/ppermute | solution.py:112
  385.7 32.3 %collective-permute-start.1 = (bf16[8,2,128,128]{3,2,0,1:T(8,128)(2,1)}, bf16[8,2,128,128]{3,2,0,1:T(8,128)(2,1)}, u32[]{:S(2)}, u32[]{:S(2)}) collective-permute-start(bf16[8,2,128,128]{3,2,0,1:T(8,128)(2,1)} %copy.156), channel_id=1, source_target_pairs={{0,1},{1,2},{2,3},{3,4},{4,5},{5,6},{6,7},{7,0},{8,9},{9,10},{10,1... | collective-permute-start | bytes 1572872 | tf_op jit(solution)/shard_map/while/body/eval_jaxpr/ppermute | solution.py:111
  431.6 24.6 %collective-permute-start.3 = (f32[8,2,128,128]{2,3,0,1:T(8,128)}, f32[8,2,128,128]{2,3,0,1:T(8,128)}, u32[]{:S(2)}, u32[]{:S(2)}) collective-permute-start(f32[8,2,128,128]{2,3,0,1:T(8,128)} %copy.38), channel_id=1, source_target_pairs={{0,1},{1,2},{2,3},{3,4},{4,5},{5,6},{6,7},{7,0},{8,9},{9,10},{10,1... | collective-permute-start | bytes 3145736 | tf_op jit(solution)/shard_map/ppermute | solution.py:119
  456.2 1195.1 %all-reduce.6.cloned.1.call-start = ((), (), s32[]{:S(2)}) async-start(), calls=%async_computation | async-start | bytes 75497472 | tf_op jit(solution)/shard_map/psum | solution.py:124
  (14 other events, 124.7 us)
Sparse Core Ops, SparseCore 0:
  456.3 600.8 all-reduce.7
  1070.6 442.7 all-reduce.5
where the time goes:
time: 1700 us; the launch traced here: 1690 us
  waiting for transfers between devices  815 us (48%)
  blocking collectives  557 us (33%)
  matrix products  166 us (10%)
  local copies, waits for them, and re-layouts  112 us (7%)
    psum x1, waiting for transfers between devices, local_program(): lax.psum(jnp.einsum('cirf,eif->cre', dq_pre, w_query, preferred_element_t...  557 us
    psum x1, blocking collectives, local_program(): attn_out = lax.psum(out_part, 'tp').astype(jnp.bfloat16)  557 us
    ppermute x7, waiting for transfers between devices, bwd_body(): dkv_blk = lax.ppermute(dkv_blk, 'cp', shift_pairs)  172 us
    ppermute x7, waiting for transfers between devices, fwd_body(): return (lax.ppermute(kv_blk, 'cp', shift_pairs), soft_stats)  56.5 us
    unnamed x26, local copies, waits for them, and re-layouts  40.3 us
    another operation x17, local copies, waits for them, and re-layouts  36.8 us
  transfers between devices with their start and end apart: 24, of which 23 were waited for; matrix products, arithmetic and copies ran while one was open for 6% of the time, Pallas kernels for 0%

commit v1 on v0

v1 whole, which is shorter than its diff:
```python
import functools
import jax
import jax.numpy as jnp
from jax import lax
from jax.experimental import pallas as pl
from jax.experimental.pallas import tpu as pltpu
from jax.sharding import PartitionSpec as P

ROWS, DEPTH, LANE, TILE, BRICK, HALF_W = 1024, 4096, 128, 256, 512, 2048
CHIPS, HEADS = 4, 8
VMEM_CAP = 66_000_000
MESH = pl.DeviceIdType.MESH
F32, BF16 = jnp.float32, jnp.bfloat16
NT = (((1,), (1,)), ((), ()))
NN = (((1,), (0,)), ((), ()))
TN = (((0,), (0,)), ((), ()))
ANY = pl.BlockSpec(memory_space=pl.ANY)
VM = pl.BlockSpec(memory_space=pltpu.VMEM)
DMA = pltpu.SemaphoreType.DMA


def dot(lhs, rhs, dims=NN):
    return lax.dot_general(lhs, rhs, dims, preferred_element_type=F32)


def win(index, size):
    start = index * size
    return pl.ds(start if isinstance(start, int) else pl.multiple_of(start, size), size)


def plane_peers(cp):
    x_of = lambda idx: idx + 2 - CHIPS * lax.rem(lax.div(idx, 2), 2)
    y_of = lambda idx: lax.rem(idx + CHIPS, HEADS)
    return x_of(cp), y_of(cp), x_of(y_of(cp)), cp + 1 - 2 * lax.rem(cp, 2)


def hand_over(src, dst, send_sem, recv_sem, tp, cp):
    return pltpu.make_async_remote_copy(src, dst, send_sem, recv_sem, device_id=(tp, cp), device_id_type=MESH)


def rope(tile, cos, sin):
    heads = [tile[:, lo:lo + LANE] for lo in range(0, tile.shape[1], LANE)]
    return [one * cos + pltpu.roll(one, LANE // 2, 1) * sin for one in heads]


def proj_kernel(q_scale, h_ref, g_ref, wq_ref, wo_ref, wk_ref, wv_ref, cos_ref, sin_ref,
                q_out, do_out, kv_out, hbuf, gbuf, wqbuf, wobuf, wkvbuf, qbuf, dobuf, kvbuf,
                load_sem, wkv_sem, osem, send_sem, recv_sem):
    tp, cp = lax.axis_index("tp"), lax.axis_index("cp")
    peers = plane_peers(cp)
    others, partner = peers[:-1], peers[-1]
    barrier = pltpu.get_barrier_semaphore()
    for peer in peers:
        pl.semaphore_signal(barrier, inc=1, device_id=(tp, peer), device_id_type=MESH)
    rows = [win(i, TILE) for i in range(CHIPS)]
    loads_h, loads_g, loads_wq, loads_wo = [
        [pltpu.make_async_copy(src.at[r], dst.at[r], load_sem.at[which, i]) for i, r in enumerate(rows)]
        for which, (src, dst) in enumerate(((h_ref, hbuf), (g_ref, gbuf), (wq_ref, wqbuf), (wo_ref, wobuf)))]
    loads_kv = [pltpu.make_async_copy(src, wkvbuf.at[:, win(i, LANE)], wkv_sem.at[i]) for i, src in enumerate((wk_ref, wv_ref))]
    for copy in loads_h[:1] + loads_kv + loads_h[1:]:
        copy.start()
    for copy in loads_h[:1] + loads_kv:
        copy.wait()
    for copy in loads_wq:
        copy.start()
    sends = []
    for i, row in enumerate(rows):
        if i:
            loads_h[i].wait()
        kv = dot(hbuf[row, :], wkvbuf[...])
        kvbuf[row, win(0, LANE)] = rope(kv[:, :LANE], cos_ref[...], sin_ref[...])[0].astype(BF16)
        kvbuf[row, win(1, LANE)] = kv[:, LANE:].astype(BF16)
        piece = kv_out.at[cp, row]
        own = pltpu.make_async_copy(kvbuf.at[row], piece, osem.at[2 + i])
        own.start()
        if i == 0:
            pl.semaphore_wait(barrier, len(peers))
        own.wait()
        sends.append([hand_over(piece, piece, send_sem.at[n, i], recv_sem.at[n, i], tp, peer) for n, peer in enumerate(peers)])
        for copy in sends[i]:
            copy.start()
    for copy in loads_wq:
        copy.wait()
    for copy in loads_g + loads_wo:
        copy.start()
    cos2, sin2 = [jnp.concatenate([tab[...]] * 2, axis=0) for tab in (cos_ref, sin_ref)]

    @pl.loop(0, HEADS)
    def _(step):
        row, col = win(lax.div(step, CHIPS), BRICK), win(lax.rem(step, CHIPS), TILE)
        tile = dot(hbuf[row, :], wqbuf[col, :], NT)
        qbuf[row, col] = (jnp.concatenate(rope(tile, cos2, sin2), axis=1) * q_scale).astype(BF16)

    store_q = pltpu.make_async_copy(qbuf, q_out, osem.at[0])
    store_q.start()
    for copy in loads_g + loads_wo:
        copy.wait()
    passes = []

    def pass_on(i):
        for n, peer in enumerate(others):
            sends[i][n].wait_recv()
            piece = kv_out.at[peer, rows[i]]
            copy = hand_over(piece, piece, send_sem.at[CHIPS + n, i], recv_sem.at[CHIPS + n, i], tp, partner)
            copy.start()
            passes.append(copy)

    for half in range(2):
        @pl.loop(half * CHIPS, (half + 1) * CHIPS)
        def _(step):
            row, col = win(lax.div(step, CHIPS), BRICK), win(lax.rem(step, CHIPS), TILE)
            dobuf[row, col] = dot(gbuf[row, :], wobuf[col, :], NT).astype(BF16)

        pass_on(half)
    store_do = pltpu.make_async_copy(dobuf, do_out, osem.at[1])
    store_do.start()
    for i in range(2, CHIPS):
        pass_on(i)
    for group in sends:
        group[-1].wait_recv()
        for copy in group:
            copy.wait_send()
    for copy in passes:
        copy.wait()
    store_q.wait()
    store_do.wait()


def projections(h, g, wq_t, wo2, wk, wv, cos_tab, sin_tab, q_scale):
    square = (ROWS, ROWS)
    kv_shape = (HEADS, ROWS, TILE)
    return pl.pallas_call(
        functools.partial(proj_kernel, q_scale),
        name="projections",
        out_shape=[jax.ShapeDtypeStruct(s, BF16) for s in (square, square, kv_shape)],
        in_specs=[ANY] * 6 + [VM] * 2,
        out_specs=[ANY] * 3,
        scratch_shapes=[pltpu.VMEM(s, BF16) for s in [(ROWS, DEPTH)] * 4 + [(DEPTH, TILE), square, square, (ROWS, TILE)]]
        + [DMA(s) for s in ((CHIPS, CHIPS), (2,), (6,), (7, CHIPS), (7, CHIPS))],
        compiler_params=pltpu.CompilerParams(collective_id=0, has_side_effects=True, vmem_limit_bytes=VMEM_CAP),
        cost_estimate=pl.CostEstimate(flops=20_000_000_000, bytes_accessed=40_000_000, transcendentals=0),
    )(h, g, wq_t, wo2, wk, wv, cos_tab, sin_tab)


def attn_kernel(q_scale, q_ref, do_ref, kv_ref, mask_ref, cos_ref, sin_ref, o_ref, dq_ref, dkv_ref):
    keys = kv_ref[:, :, :LANE].reshape(ROWS, LANE)
    vals = kv_ref[:, :, LANE:].reshape(ROWS, LANE)
    sums = []
    for pair in range(CHIPS):
        cols = [win(2 * pair + i, LANE) for i in range(2)]
        q = jnp.concatenate([q_ref[:, c] for c in cols], axis=0)
        do = jnp.concatenate([do_ref[:, c] for c in cols], axis=0)
        scores = dot(q, keys, NT) + mask_ref[...]
        prob = jnp.exp(scores - jnp.max(scores, axis=1, keepdims=True))
        prob = prob * (1.0 / jnp.sum(prob, axis=1, keepdims=True))
        prob_b = prob.astype(BF16)
        out = dot(prob_b, vals).astype(BF16)
        delta = jnp.sum(do.astype(F32) * out.astype(F32), axis=1, keepdims=True)
        d_score = (prob * (dot(do, vals, NT) - delta)).astype(BF16)
        dq = dot(d_score, keys)
        dq = ((dq * cos_ref[...] - pltpu.roll(dq, LANE // 2, 1) * sin_ref[...]) * q_scale).astype(BF16)
        for i, c in enumerate(cols):
            o_ref[:, c] = out[i * LANE:(i + 1) * LANE]
            dq_ref[:, c] = dq[i * LANE:(i + 1) * LANE]
        sums.append((dot(q.T, d_score), dot(do.T, prob_b)))
    for kind, parts in enumerate(zip(*sums)):
        total = (parts[0] + parts[1]) + (parts[2] + parts[3])
        for j in range(HEADS):
            dkv_ref[j, kind] = total[:, j * LANE:(j + 1) * LANE]


def attention(q, do, kv, mask2, cos_tab, sin_tab, q_scale):
    row_block = pl.BlockSpec((LANE, ROWS), lambda b: (b, 0))
    whole = lambda a: pl.BlockSpec(a.shape, lambda b: (0,) * a.ndim)
    return pl.pallas_call(
        functools.partial(attn_kernel, q_scale),
        name="attention",
        grid=(HEADS,),
        out_shape=[jax.ShapeDtypeStruct((ROWS, ROWS), BF16)] * 2 + [jax.ShapeDtypeStruct((HEADS, 2, TILE, BRICK), F32)],
        in_specs=[row_block, row_block, pl.BlockSpec((HEADS, LANE, TILE), lambda b: (0, b, 0)), whole(mask2), whole(cos_tab), whole(sin_tab)],
        out_specs=[row_block, row_block, pl.BlockSpec((HEADS, 2, LANE, LANE), lambda b: (0, 0, lax.div(b, CHIPS), lax.rem(b, CHIPS)))],
        compiler_params=pltpu.CompilerParams(vmem_limit_bytes=VMEM_CAP),
        cost_estimate=pl.CostEstimate(flops=30_000_000_000, bytes_accessed=20_000_000, transcendentals=8_000_000),
    )(q, do, kv, mask2, cos_tab, sin_tab)


def tables(cp):
    half = LANE // 2
    pos = cp * LANE + jnp.arange(LANE)
    inv_freq = 1.0 / jnp.power(10000.0, jnp.arange(half, dtype=F32) * (2.0 / LANE))
    ang = pos.astype(F32)[:, None] * inv_freq[None, :]
    cos, sin = jnp.cos(ang), jnp.sin(ang)
    double = lambda tab: jnp.tile(tab, (2, 1))
    mask = jnp.where(jnp.arange(ROWS)[None, :] <= pos[:, None], 0.0, -jnp.inf).astype(F32)
    return jnp.concatenate([cos.T, sin.T], axis=0), double(jnp.concatenate([cos, cos], axis=1)), double(jnp.concatenate([-sin, sin], axis=1)), double(mask)


DKV, DWO, DWQ, DWKV = 0, (1, 2), (3, 4), 5
SETS, SLOTS, GROUPS = 6, 5, 8
LEADS, EARLY = (1, 3), 2
FAR_ROLES = (0, 2, 3)
INPUTS = ("o", "dq", "wo", "wq", "near", "mid", "far", "wkv", "g", "h", "dkv", "tabs")
OUTPUTS = {"out": ((ROWS, DEPTH), BF16), "dh": ((ROWS, DEPTH), BF16), "dwo": ((ROWS, DEPTH), F32), "dwq": ((DEPTH, ROWS), F32),
           "dwkv": ((DEPTH, TILE), F32), "dkvb": ((ROWS, TILE), BF16), "wland": ((DEPTH, HALF_W), BF16),
           "pland": ((SETS, CHIPS, BRICK, BRICK), F32), "xland": ((SETS, 2, BRICK, BRICK), F32), "hland": ((SETS, 2, TILE, BRICK), F32), "zland": ((2, BRICK, BRICK), F32)}
BUFFERS = {"abuf": ((ROWS, DEPTH + TILE), BF16), "wa": ((DEPTH + TILE, HALF_W), BF16), "wb": ((DEPTH + TILE, TILE), BF16),
           "tile_a": ((LANE, HALF_W), BF16), "tile_b": ((ROWS, TILE), BF16), "keep": ((SLOTS, CHIPS, BRICK, BRICK), F32),
           "tmp": ((CHIPS, BRICK, BRICK), F32), "stage": ((2, BRICK, BRICK), F32), "left": ((2, ROWS, BRICK), BF16),
           "right": ((2, ROWS, BRICK), BF16), "zbuf": ((BRICK, BRICK), F32)}
SEMS = {"load": (12,), "early": (4,), "asend": (2, GROUPS), "arecv": (2, 3, GROUPS), "wsend": (2, GROUPS), "wrecv": (2, 3, GROUPS), "fsend": (2, 3), "frecv": (2, 3, GROUPS),
        "rsend": (2, 2, 2, GROUPS), "rrecv": (2, 2, GROUPS), "swsend": (3,), "swrecv": (3,), "dsend": (SETS, CHIPS), "drecv": (SETS, CHIPS),
        "xsend": (SETS, 2), "xrecv": (SETS, 2), "hsend": (SETS, 2), "hrecv": (SETS, 2), "zsend": (3,), "zrecv": (3,), "gsend": (SETS, 9), "grecv": (SETS, 9)}


class Exchange:
    def __init__(self, *refs):
        for name, ref in zip((*INPUTS, *OUTPUTS, *BUFFERS, *SEMS, "credit"), refs):
            setattr(self, name, ref)
        self.tp, self.cp = lax.axis_index("tp"), lax.axis_index("cp")
        self.core, self.chip = lax.rem(self.cp, 2), lax.div(self.cp, 2)
        self.x, self.y, self.diag, self.partner = plane_peers(self.cp)
        self.acts, self.weights, self.results = (self.o, self.dq), (self.wo, self.wq), (self.out, self.dh)

    def move(self, pairs):
        copies = [pltpu.make_async_copy(src, dst, self.load.at[i]) for i, (src, dst) in enumerate(pairs)]
        for copy in copies:
            copy.start()
        for copy in copies:
            copy.wait()


    def plane(self, phase, role):
        return CHIPS - 1 - role if phase else role

    def role(self, phase):
        return self.plane(phase, self.tp)

    def act_copy(self, phase, src, i, to):
        row = win(i, LANE)
        return hand_over(self.acts[phase].at[row], self.abuf.at[row, win(src, ROWS)], self.asend.at[phase, i],
                         self.arecv.at[phase, FAR_ROLES.index(src), i], to, self.cp)

    def w_copy(self, phase, src, n, to):
        rows = 2 * src + self.core
        return hand_over(self.weights[phase].at[win(self.core, BRICK), win(GROUPS + n, TILE)], self.wland.at[win(rows, BRICK), win(n, TILE)],
                         self.wsend.at[phase, n], self.wrecv.at[phase, FAR_ROLES.index(src), n], to, self.cp)

    def cross_copy(self, phase, src, n, core):
        place = self.wland.at[win(2 * src + core, BRICK), win(n, TILE)]
        slot = FAR_ROLES.index(src)
        return hand_over(place, place, self.fsend.at[phase, slot], self.frecv.at[phase, slot, n], self.tp, self.partner)

    def piece(self, phase, kind, idx):
        if kind:
            return self.results[phase].at[:, win(GROUPS + idx, TILE)]
        return self.results[phase].at[win(idx, LANE), win(0, HALF_W)]

    def result_copy(self, phase, kind, idx, way, to_role):
        piece = self.piece(phase, kind, idx)
        return hand_over(piece, piece, self.rsend.at[phase, way, kind, idx], self.rrecv.at[phase, kind, idx], self.plane(phase, to_role), self.cp)

    def ask_far(self, phase):
        pl.semaphore_signal(self.credit.at[phase], inc=1, device_id=(self.plane(phase, 3), self.cp), device_id_type=MESH)

    def multiply(self, phase, kind, idx):
        depth = pl.ds(0, DEPTH + TILE * phase)
        act, weight = self.acts[phase], self.weights[phase]
        if kind == 0:
            row = win(idx, LANE)
            for src in FAR_ROLES:
                self.act_copy(phase, src, idx, self.plane(phase, src)).wait_recv()
            self.ask_far(phase)

            @pl.loop(0, CHIPS)
            def _(i):
                col = win(i, BRICK)
                self.tile_a[:, col] = dot(self.abuf[row, depth], self.wa[depth, col]).astype(BF16)
        else:
            for src in FAR_ROLES:
                self.cross_copy(phase, src, idx, 1 - self.core).wait_recv()
                self.cross_copy(phase, src, idx, self.core).wait_send()
            pairs = [(self.wland.at[win(src, ROWS), win(idx, TILE)], self.wb.at[win(src, ROWS)]) for src in FAR_ROLES]
            pairs.append((weight.at[:, win(GROUPS + idx, TILE)], self.wb.at[win(1, ROWS)]))
            if phase:
                pairs.append((self.wkv.at[:, win(GROUPS + idx, TILE)], self.wb.at[pl.ds(DEPTH, TILE)]))
            self.move(pairs)

            @pl.loop(0, CHIPS)
            def _(i):
                row = win(i, TILE)
                self.tile_b[row, :] = dot(self.abuf[row, depth], self.wb[depth, :]).astype(BF16)

        self.move([(self.tile_b if kind else self.tile_a, self.piece(phase, kind, idx))])
        for way, to_role in enumerate((0, 2)):
            self.result_copy(phase, kind, idx, way, to_role).start()

    def swap_weights(self, phase, idx):
        @pl.when(self.role(phase) == 1)
        def _():
            for src in FAR_ROLES:
                self.w_copy(phase, src, idx, self.plane(phase, src)).wait_recv()
                self.cross_copy(phase, src, idx, self.core).start()

            @pl.when(idx < GROUPS - LEADS[phase])
            def _():
                self.ask_far(phase)

    def group(self, phase, kind, idx):
        role = self.role(phase)

        @pl.when(role == 0)
        def _():
            self.result_copy(phase, kind, idx, 0, 1).wait_recv()

        @pl.when(role == 1)
        def _():
            self.multiply(phase, kind, idx)

        @pl.when(role == 2)
        def _():
            self.result_copy(phase, kind, idx, 0, 1).wait_recv()
            self.result_copy(phase, kind, idx, 0, 3).start()

        item = idx + LEADS[phase]

        @pl.when((role == 3) & ((item < GROUPS) | (kind == 0)))
        def _():
            pl.semaphore_wait(self.credit.at[phase], 1)

            @pl.when((item < GROUPS) & (kind == 0))
            def _():
                self.act_copy(phase, 3, item, self.plane(phase, 1)).start()

            @pl.when((item >= GROUPS) | (kind == 1))
            def _():
                self.w_copy(phase, 3, lax.rem(item, GROUPS), self.plane(phase, 1)).start()

    def feed(self, phase, src, acts, weights):
        @pl.when(self.role(phase) == src)
        def _():
            for i in acts:
                self.act_copy(phase, src, i, self.plane(phase, 1)).start()
            for n in weights:
                self.w_copy(phase, src, n, self.plane(phase, 1)).start()

    def start_line(self):
        for phase in range(2):
            @pl.when(self.role(phase) == 1)
            def _():
                swaps = []
                for i, (half, src) in enumerate(zip((self.near, self.mid, self.far), FAR_ROLES)):
                    swaps.append(hand_over(half, self.wa.at[win(2 * src + self.core, BRICK)], self.swsend.at[i], self.swrecv.at[i], self.tp, self.partner))
                    swaps[i].start()
                pairs = [(half, self.wa.at[win(2 * src + self.core, BRICK)]) for half, src in zip((self.near, self.mid, self.far), FAR_ROLES)]
                pairs.append((self.weights[phase].at[:, win(0, HALF_W)], self.wa.at[win(1, ROWS)]))
                pairs.append((self.acts[phase], self.abuf.at[:, win(1, ROWS)]))
                pairs.append((self.wkv.at[:, win(0, HALF_W)], self.wa.at[pl.ds(DEPTH, TILE)]))
                self.move(pairs)

    def end_swap(self):
        @pl.when((self.tp == 1) | (self.tp == 2))
        def _():
            for i, (half, src) in enumerate(zip((self.near, self.mid, self.far), FAR_ROLES)):
                hand_over(half, self.wa.at[win(2 * src + 1 - self.core, BRICK)], self.swsend.at[i], self.swrecv.at[i], self.tp, self.partner).wait()

    def end_line(self):
        for phase in range(2):
            role = self.role(phase)
            for kind in range(2):
                @pl.when(role == 1)
                def _():
                    @pl.loop(0, GROUPS)
                    def _(idx):
                        for way, to_role in enumerate((0, 2)):
                            self.result_copy(phase, kind, idx, way, to_role).wait_send()

                @pl.when(role == 2)
                def _():
                    @pl.loop(0, GROUPS)
                    def _(idx):
                        self.result_copy(phase, kind, idx, 0, 3).wait_send()

                @pl.when(role == 3)
                def _():
                    @pl.loop(0, GROUPS)
                    def _(idx):
                        self.result_copy(phase, kind, idx, 0, 2).wait_recv()

            for src in FAR_ROLES:
                @pl.when(role == src)
                def _():
                    for i in range(GROUPS):
                        self.act_copy(phase, src, i, self.plane(phase, 1)).wait_send()
                        self.w_copy(phase, src, i, self.plane(phase, 1)).wait_send()


    def brick(self, which, ref):
        return ref.at[:, pl.ds(0, TILE)] if which == DWKV else ref

    def pair_copy(self, kind, i, src, which=None):
        which = kind if which is None else which
        return hand_over(src, self.brick(kind, self.pland.at[which, i]), self.dsend.at[which, i], self.drecv.at[which, i], self.tp, self.partner)

    def chip_copies(self, which):
        return [hand_over(self.brick(which, self.keep.at[which % SLOTS, lax.div(peer, 2)]), self.brick(which, self.xland.at[which, n]),
                          self.xsend.at[which, n], self.xrecv.at[which, n], self.tp, peer) for n, peer in enumerate((self.x, self.y))]

    def half_copies(self, which):
        block = self.brick(which, self.keep.at[which % SLOTS, lax.div(self.diag, 2)])
        return [hand_over(block.at[win(n, TILE)], self.brick(which, self.hland.at[which, n]),
                          self.hsend.at[which, n], self.hrecv.at[which, n], self.tp, peer) for n, peer in enumerate((self.x, self.y))]

    def own_blocks(self):
        return [pltpu.make_async_copy(self.dkv.at[2 * i + self.core], self.keep.at[0, i], self.early.at[i]) for i in range(CHIPS)]

    def hand_dkv(self):
        for i in range(CHIPS):
            self.pair_copy(DKV, i, self.dkv.at[2 * i + 1 - self.core]).start()
        for copy in self.own_blocks():
            copy.start()

    def fetch(self, part):
        half, i = win(lax.rem(lax.div(part, CHIPS), 2), BRICK), lax.rem(part, CHIPS)
        narrow = pl.ds(0, TILE)
        for n, block in enumerate((2 * i + 1 - self.core, 2 * i + self.core)):
            block = win(block, BRICK)
            right = self.right.at[n]
            for kind, pair in enumerate((((self.o.at[:, half], self.left.at[n]), (self.g.at[:, block], right)),
                                         ((self.h.at[:, block], self.left.at[n]), (self.dq.at[:, half], right)),
                                         ((self.h.at[:, block], self.left.at[n]), (self.dkvb, right.at[:, narrow])))):
                @pl.when(lax.div(part, 2 * CHIPS) == kind)
                def _():
                    for m, (src, dst) in enumerate(pair):
                        pltpu.make_async_copy(src, dst, self.early.at[2 * n + m]).start()

    def make(self, part, which=None):
        kind, i = which, lax.rem(part, CHIPS)
        which = 1 + lax.div(part, CHIPS) if which is None else which
        col = pl.ds(0, BRICK if kind is None else TILE)
        slot = self.stage.at[lax.rem(part, 2), :, col]

        @pl.when(i > 1)
        def _():
            self.pair_copy(kind, i - 2, slot, which).wait_send()

        for n, dst in enumerate((slot, self.keep.at[lax.rem(which, SLOTS), i, :, col])):
            left, right = self.left.at[n], self.right.at[n, :, col]
            for m, factor in enumerate((left, right)):
                pltpu.make_async_copy(self.h.at[:, col] if m else self.h.at[:, win(0, BRICK)], factor, self.early.at[2 * n + m]).wait()
            dst[...] = dot(left[...], right[...], TN)
            if n == 0:
                self.pair_copy(kind, i, slot, which).start()

        @pl.when((part != PARTS - 1) & (part != PARTS + CHIPS - 1))
        def _():
            self.fetch(part + 1)

    def total(self, which, count, add):
        @pl.loop(0, count * HEADS)
        def _(step):
            add(lax.div(step, HEADS), win(lax.rem(step, HEADS), LANE // 2))

    def add_pair(self, which):
        keep = self.keep.at[which % SLOTS]
        landed = [self.brick(which, self.pland.at[which, i]) for i in range(CHIPS)]
        for i in range(CHIPS):
            self.pair_copy(which, i, landed[i]).wait_recv()
        for i in range(0 if which == DKV else CHIPS // 2, CHIPS):
            self.pair_copy(which, i, landed[i]).wait_send()
        if which == DKV:
            for copy in self.own_blocks():
                copy.wait()
            self.fetch(0)
        self.move([(landed[i], self.brick(which, self.tmp.at[i])) for i in range(CHIPS)])
        col = pl.ds(0, TILE if which == DWKV else BRICK)

        def add(i, row):
            keep[i, row, col] = keep[i, row, col] + self.tmp[i, row, col]

        self.total(which, CHIPS, add)
        for copy in self.half_copies(which):
            copy.start()

    def relay(self, which):
        for copy in self.half_copies(which):
            copy.wait()
        self.move([(self.brick(which, self.hland.at[which, n]), self.brick(which, self.tmp.at[n, win(0, TILE)])) for n in range(2)])
        col = pl.ds(0, TILE if which == DWKV else BRICK)
        for n, peer in enumerate((self.y, self.x)):
            block = self.keep.at[which % SLOTS, lax.div(peer, 2)]
            for step in range(CHIPS):
                row, src = win(CHIPS * n + step, LANE // 2), win(step, LANE // 2)
                block[row, col] = block[row, col] + self.tmp[n, src, col]
        for copy in self.chip_copies(which):
            copy.start()

    def place(self, which, owner):
        if which in DWO:
            return self.dwo.at[win(which - DWO[0], BRICK), win(owner, BRICK)]
        if which in DWQ:
            return self.dwq.at[win(owner, BRICK), win(which - DWQ[0], BRICK)]
        return self.dwkv.at[win(owner, BRICK)]

    def share_copy(self, which, kind):
        owner = (self.cp, self.cp, self.cp, self.x, self.y, self.y, self.x, self.diag, self.diag)[kind]
        to = (self.x, self.y, self.partner, self.partner, self.partner, self.x, self.y, self.partner, self.partner)[kind]
        place = self.place(which, owner)
        if kind > 4:
            place = place.at[win((kind + 1) % 2, TILE)]
        return hand_over(place, place, self.gsend.at[which, kind], self.grecv.at[which, kind], self.tp, to)

    def shared_place(self, which, kind):
        mate = lambda idx: plane_peers(idx)[-1]
        owner = (self.x, self.y, self.partner, mate(self.x), mate(self.y), self.diag, self.diag, mate(self.diag), mate(self.diag))[kind]
        place = self.place(which, owner)
        if kind > 4:
            place = place.at[win((kind + 1) % 2, TILE)]
        return hand_over(place, place, self.gsend.at[which, kind], self.grecv.at[which, kind], self.tp, self.partner)

    def add_chips(self, which):
        copies = self.chip_copies(which)
        for copy in copies:
            copy.wait()
        self.move([(self.brick(which, self.xland.at[which, n]), self.brick(which, self.tmp.at[n])) for n in range(len(copies))])
        col = pl.ds(0, TILE if which == DWKV else BRICK)
        own = self.keep.at[which % SLOTS, self.chip]

        def add(_, row):
            own[row, col] = own[row, col] + (self.tmp[0, row, col] + self.tmp[1, row, col])

        self.total(which, 1, add)
        if which == DKV:
            self.total(which, 1, self.keep_z)
            for end, inner in ((0, 1), (3, 2)):
                @pl.when(self.tp == end)
                def _():
                    self.z_copy(0, inner).start()
            return
        self.move([(self.brick(which, own), self.place(which, self.cp))])
        for kind in range(3):
            self.share_copy(which, kind).start()

    def pass_on(self, which):
        for kind in range(2):
            self.shared_place(which, kind).wait_recv()
        for kind in (5, 6, 3, 4):
            self.share_copy(which, kind).start()

    def pass_diagonal(self, which):
        for kind in (5, 6):
            self.shared_place(which, kind).wait_recv()
        for kind in (7, 8):
            self.share_copy(which, kind).start()

    def end_share(self, which):
        for kind in (2, 3, 4, 7, 8):
            self.shared_place(which, kind).wait_recv()
        for kind in range(9):
            self.share_copy(which, kind).wait_send()


    def keep_z(self, _, row):
        self.zbuf[row] = self.keep[0, self.chip, row]

    def z_copy(self, slot, to):
        return hand_over(self.zbuf, self.zland.at[slot], self.zsend.at[slot], self.zrecv.at[slot], to, self.cp)

    def z_result(self, slot, to):
        return hand_over(self.dkvb, self.dkvb, self.zsend.at[slot], self.zrecv.at[2], to, self.cp)

    def meet(self):
        for inner in (1, 2):
            @pl.when(self.tp == inner)
            def _():
                self.z_copy(0, CHIPS - 1 - inner).wait_recv()
                self.move([(self.zland.at[0], self.tmp.at[0])])

                def add(_, row):
                    self.zbuf[row] = self.zbuf[row] + self.tmp[0, row]

                self.total(DKV, 1, add)
                if inner == 2:
                    self.z_copy(1, 1).start()

    def settle(self):
        half = LANE // 2

        @pl.when(self.tp == 1)
        def _():
            self.z_copy(1, 2).wait_recv()
            self.move([(self.zland.at[1], self.tmp.at[0]), (self.tabs, self.tmp.at[1, win(0, LANE), win(0, LANE)])])
            for b in range(HEADS):
                cos, sin = self.tmp[1, win(0, half), win(0, LANE)], self.tmp[1, win(1, half), win(0, LANE)]
                for kind in range(2):
                    row, col = win(2 * kind + b // CHIPS, LANE), win(b % CHIPS, LANE)
                    part = self.zbuf[row, col] + self.tmp[0, row, col]
                    if kind == 0:
                        low, high = part[:half], part[half:]
                        part = jnp.concatenate([low * cos + high * sin, high * cos - low * sin], axis=0)
                    self.abuf[win(b, LANE), win(DEPTH // LANE + kind, LANE)] = part.T.astype(BF16)
            self.move([(self.abuf.at[:, pl.ds(DEPTH, TILE)], self.dkvb)])
            self.z_result(2, 2).start()
            self.z_result(0, 0).start()

    def take(self):
        @pl.when(self.tp == 2)
        def _():
            self.z_result(2, 1).wait_recv()
            self.z_result(2, 3).start()
            self.move([(self.dkvb, self.abuf.at[:, pl.ds(DEPTH, TILE)])])

    def get_result(self):
        for end in (0, 3):
            @pl.when(self.tp == end)
            def _():
                self.z_result(2, 1).wait_recv()
                self.z_copy(0, 1).wait_send()

        @pl.when(self.tp == 1)
        def _():
            self.z_result(0, 0).wait_send()

        @pl.when(self.tp == 2)
        def _():
            self.z_copy(1, 1).wait_send()

        @pl.when((self.tp == 1) | (self.tp == 2))
        def _():
            self.z_result(2, 3).wait_send()

        self.fetch(PARTS)


STEPS = {"add_pair": ((1, 3, 5, 7, 9, 22), (1, 5, 9, 13, 17, 23)), "relay": ((3, 6, 7, 10, 13, 24), (4, 8, 12, 16, 20, 25)),
         "add_chips": ((6, 10, 13, 15, 18, 26), (7, 11, 15, 19, 23, 28)), "pass_on": ((0, 25, 26, 27, 28, 29), (0, 15, 19, 23, 27, 30)),
         "pass_diagonal": ((0, 28, 29, 30, 31, 31), (0, 19, 23, 27, 31, 31))}
ONCE = {"hand_dkv": 0, "meet": 10, "settle": 15, "get_result": 17}
PARTS, LATE = 16, 18


def exchange_kernel(*refs):
    dev = Exchange(*refs)
    barrier = pltpu.get_barrier_semaphore()
    for step in range(1, CHIPS):
        pl.semaphore_signal(barrier, inc=1, device_id=(lax.rem(dev.tp + step, CHIPS), dev.cp), device_id_type=MESH)
    for peer in plane_peers(dev.cp):
        pl.semaphore_signal(barrier, inc=1, device_id=(dev.tp, peer), device_id_type=MESH)
    pl.semaphore_wait(barrier, 7)
    blocks = range(GROUPS)
    dev.feed(0, 3, blocks[:LEADS[0]], ())
    dev.feed(0, 0, blocks[:1], ())
    for i in blocks[1:]:
        dev.feed(0, 0, (i,), ())
        if i <= LEADS[1]:
            dev.feed(1, 3, (i - 1,), ())
    dev.feed(0, 0, (), blocks)
    dev.feed(0, 2, blocks, blocks)
    dev.feed(1, 2, blocks[:EARLY], ())
    dev.start_line()
    dev.end_swap()
    busy = dev.tp == 2

    @pl.loop(0, CHIPS * GROUPS)
    def _(now):
        idx = lax.rem(now, GROUPS)
        spans = [(lax.div(now, GROUPS) == 2 * phase + kind, phase, kind) for phase in range(2) for kind in range(2)]

        @pl.when(now == 2 * GROUPS)
        def _():
            dev.feed(1, 0, blocks, blocks)
            dev.feed(1, 2, blocks[EARLY:], blocks)
            dev.take()

        for here, phase, kind in spans:
            @pl.when(here)
            def _():
                if kind:
                    dev.swap_weights(phase, idx)
                else:
                    dev.group(phase, kind, idx)

        for step, at in ONCE.items():
            @pl.when(now == at)
            def _():
                getattr(dev, step)()

        for step, (early, late) in STEPS.items():
            for which in range(SETS):
                if late[which]:
                    @pl.when(now == jnp.where(busy, early[which], late[which]))
                    def _():
                        getattr(dev, step)(which)

        @pl.loop(jnp.where(busy, jnp.maximum(2 * now - 2, 0), jnp.maximum(now - 1, 0)), jnp.minimum(jnp.where(busy, 2 * now, now), PARTS))
        def _(part):
            dev.make(part)

        @pl.when((now >= LATE) & (now < LATE + CHIPS))
        def _():
            dev.make(now + PARTS - LATE, DWKV)

        for here, phase, kind in spans:
            if kind:
                @pl.when(here)
                def _():
                    dev.group(phase, kind, idx)

    for which in range(1, SETS):
        dev.end_share(which)
    dev.end_line()


def exchange(*operands):
    return pl.pallas_call(
        exchange_kernel,
        name="exchange",
        out_shape=[jax.ShapeDtypeStruct(*spec) for spec in OUTPUTS.values()],
        in_specs=[ANY] * len(operands),
        out_specs=[ANY] * len(OUTPUTS),
        scratch_shapes=[pltpu.VMEM(*spec) for spec in BUFFERS.values()] + [DMA(shape) for shape in SEMS.values()] + [pltpu.SemaphoreType.REGULAR((2,))],
        compiler_params=pltpu.CompilerParams(collective_id=1, has_side_effects=True, vmem_limit_bytes=VMEM_CAP),
        cost_estimate=pl.CostEstimate(flops=300_000_000_000, bytes_accessed=200_000_000, transcendentals=0),
    )(*operands)


def solution(mesh):
    def local_program(hidden, grad_out, w_query, w_key, w_value, w_out):
        tp, cp = lax.axis_index("tp"), lax.axis_index("cp")
        h, g = hidden.reshape(ROWS, DEPTH), grad_out.reshape(ROWS, DEPTH)
        q_scale = LANE ** -0.5
        tabs, cos_tab, sin_tab, mask2 = tables(cp)
        wo2 = w_out.reshape(ROWS, DEPTH)
        wq_t = w_query.transpose(1, 2, 0).reshape(ROWS, DEPTH)
        wkv_t = jnp.concatenate([w_key, w_value], axis=1).T
        wo_half, wq_half = [lax.dynamic_slice(w, (lax.rem(cp, 2) * BRICK, 0), (BRICK, HALF_W)) for w in (wo2, wq_t)]
        one_way, other_way = jnp.where(tp <= 1, wo_half, wq_half), jnp.where(tp <= 1, wq_half, wo_half)
        near = lax.ppermute(one_way, "tp", [(0, 1), (3, 2)])
        mid = lax.ppermute(other_way, "tp", [(2, 1), (1, 2)])
        far = lax.ppermute(other_way, "tp", [(3, 1), (0, 2)])
        q, d_o, kv = projections(h, g, wq_t, wo2, w_key, w_value, cos_tab, sin_tab, q_scale)
        o, dq, dkv = attention(q, d_o, kv, mask2, cos_tab, sin_tab, q_scale)
        out, dh, dwo, dwq, dwkv = exchange(o, dq, wo2, wq_t, near, mid, far, wkv_t, g, h, dkv.reshape(HEADS, BRICK, BRICK), tabs)[:5]
        return (out.reshape(hidden.shape), dh.reshape(hidden.shape), dwq.reshape(w_query.shape),
                dwkv[:, :LANE], dwkv[:, LANE:], dwo.reshape(w_out.shape))

    row_spec, head_spec = P(None, "cp", None), P("tp", None, None)
    query_spec = P(None, "tp", None)
    return jax.shard_map(local_program, mesh=mesh, in_specs=(row_spec, row_spec, query_spec, P(), P(), head_spec),
                         out_specs=(row_spec, row_spec, query_spec, P(), P(), head_spec), check_vma=False)
```

time: 1700 us -> 612 us (0.36)
  waiting for transfers between devices: 815 us -> 2.71 us
  blocking collectives: 557 us -> 0 us
  Pallas kernels: 0 us -> 524 us
  matrix products: 166 us -> 0 us
  local copies, waits for them, and re-layouts: 112 us -> 62.7 us
    psum x2 -> x0, waiting for transfers between devices: 557 us -> none  [the longest x1 557 us: local_program(): lax.psum(jnp.einsum('cirf,eif->cre', dq_pre, w_query, preferred_element_t...]
    psum x1 -> x0, blocking collectives: 557 us -> none  [local_program(): attn_out = lax.psum(out_part, 'tp').astype(jnp.bfloat16)]
    pallas_call x0 -> x3, Pallas kernels: none -> 524 us  [the longest x1 450 us: exchange(): pl.pallas_call(exchange_kernel, name='exchange', out_shape=[jax.ShapeDtyp...]
    ppermute x22 -> x3, waiting for transfers between devices: 258 us -> 2.71 us  [the longest x1 2.71 us: local_program(): near = lax.ppermute(one_way, 'tp', [(0, 1), (3, 2)])]
    dot_general x19 -> x0, matrix products: 166 us -> none  [the longest x1 27.1 us: local_program(): jnp.einsum('bsd,dhe->bhse', hidden, w_query, preferred_element_type=jnp.f...]
    another operation x17 -> x3, local copies, waits for them, and re-layouts: 36.8 us -> 2.48 us  [tables(): double = lambda tab: jnp.tile(tab, (2, 1))]
    while x10 -> x0, local copies, waits for them, and re-layouts: 22.8 us -> none
    unnamed x26 -> x8, local copies, waits for them, and re-layouts: 40.3 us -> 43.7 us
  transfers between devices with their start and end apart: 24 -> 3, of which waited for: 23 -> 1; matrix products, arithmetic and copies ran while one was open for 6% -> 1% of each run, Pallas kernels for 0% -> 12%
where the time goes in v1:
time: 612 us; the launch traced here: 611 us
  Pallas kernels  524 us (86%)
  local copies, waits for them, and re-layouts  62.7 us (10%)
  starting transfers between devices  11.9 us (2%)
  other arithmetic  8.56 us (1%)
    pallas_call x1, Pallas kernels, exchange(): pl.pallas_call(exchange_kernel, name='exchange', out_shape=[jax.ShapeDtyp...  450 us
    unnamed x8, local copies, waits for them, and re-layouts  43.7 us
    pallas_call x1, Pallas kernels, attention(): pl.pallas_call(functools.partial(attn_kernel, q_scale), name='attention',...  37.4 us
    pallas_call x1, Pallas kernels, projections(): pl.pallas_call(functools.partial(proj_kernel, q_scale), name='projections...  36.5 us
  transfers between devices with their start and end apart: 3, of which 1 were waited for; matrix products, arithmetic and copies ran while one was open for 1% of the time, Pallas kernels for 12%

profile of v1, /device:TPU:0, one launch (start us, length us, event | category | flops | bytes accessed | tf_op | source)
XLA Modules:
  0.0 610.6 jit_solution(13828265575310529856)
XLA Ops:
  0.6 12.1 %copy.12 = bf16[8,128,4096]{2,1,0:T(8,128)(2,1)} copy(bf16[8,128,4096]{1,0,2:T(8,128)(2,1)} %bitcast.22) | data formatting | bytes 16777216 | tf_op jit(solution)/shard_map/transpose | solution.py:733
  12.7 5.7 broadcast_select_fusion
  18.4 7.3 %collective-permute-start.2 = (bf16[512,2048]{1,0:T(8,128)(2,1)}, bf16[512,2048]{1,0:T(8,128)(2,1)}, u32[]{:S(2)}, u32[]{:S(2)}) collective-permute-start(bf16[512,2048]{1,0:T(8,128)(2,1)} %get-tuple-element.28), channel_id=1, source_target_pairs={{24,8},{0,16},{25,9},{1,17},{26,10},{2,18},{27,11},{3,19},{28,12},... | collective-permute-start | bytes 6291464 | tf_op jit(solution)/shard_map/ppermute | solution.py:739
  25.7 2.0 collective-permute-start.1
  27.6 2.6 collective-permute-start
  30.2 0.2 multiply_cosine_fusion.1
  30.5 0.3 fusion.1
  30.9 0.1 fusion
  31.0 0.5 copy.13
  31.5 1.5 copy.14
  33.0 0.6 pad_maximum_fusion.2.refs_11_
  33.7 1.5 maximum_bitcast_fusion.refs_7_
  35.2 0.7 tile.14
  35.8 0.7 tile.12
  36.5 36.5 %projections.1 = (bf16[1024,1024]{1,0:T(8,128)(2,1)}, bf16[1024,1024]{1,0:T(8,128)(2,1)}, bf16[8,1024,256]{2,1,0:T(8,128)(2,1)}) custom-call(bf16[1024,4096]{1,0:T(8,128)(2,1)} %bitcast.33, bf16[1024,4096]{1,0:T(8,128)(2,1)} %bitcast.35, bf16[1024,4096]{1,0:T(8,128)(2,1)} %bitcast.20, bf16[1024,4096]{1,0:T(8,128)(2,1)} %bitcast.27, ...), custom_call_target="tpu_custom_call" | custom-call | flops 20000000000 | bytes 40000000 | tf_op jit(solution)/shard_map/projections/pallas_call | solution.py:132
  73.0 1.2 tile.31
  74.2 37.4 %attention.1 = (bf16[1024,1024]{1,0:T(8,128)(2,1)}, bf16[1024,1024]{1,0:T(8,128)(2,1)}, f32[8,2,256,512]{3,2,1,0:T(8,128)}) custom-call(bf16[1024,1024]{1,0:T(8,128)(2,1)} %get-tuple-element.17.q_ref, bf16[1024,1024]{1,0:T(8,128)(2,1)} %get-tuple-element.18.do_ref, bf16[8,1024,256]{2,1,0:T(8,128)(2,1)} %get-tuple-element.19.kv_ref, f32[256,1024]{1,0:T(8,128)} %bitcast.25, ...), custom_call_target="tpu_custom_call" | custom-call | flops 30000001024 | bytes 20000000 | tf_op jit(solution)/shard_map/attention/pallas_call | solution.py:175
  111.6 2.7 collective-permute-done.refs_4_
  114.3 450.1 %exchange.1 = (bf16[1024,4096]{1,0:T(8,128)(2,1)}, bf16[1024,4096]{1,0:T(8,128)(2,1)}, f32[1024,4096]{1,0:T(8,128)}, f32[4096,1024]{1,0:T(8,128)}, f32[4096,256]...) custom-call(bf16[1024,1024]{1,0:T(8,128)(2,1)} %get-tuple-element.20, ...), custom_call_target="tpu_custom_call" | custom-call | flops 299999985664 | bytes 200000000 | tf_op jit(solution)/shard_map/exchange/pallas_call | solution.py:714
  564.4 4.5 fusion.3
  568.9 14.2 %copy.15 = f32[512,8,8,128]{3,2,1,0:T(8,128)} copy(f32[512,8,8,128]{3,1,2,0:T(8,128)} %bitcast.17) | data formatting | bytes 33554432
  583.1 7.9 %copy.19 = bf16[8,128,4096]{2,1,0:T(8,128)(2,1)} copy(bf16[8,128,4096]{2,1,0:T(8,128)(2,1)} %bitcast.24) | data formatting | bytes 16777216
  591.0 7.9 %copy.20 = bf16[8,128,4096]{2,1,0:T(8,128)(2,1)} copy(bf16[8,128,4096]{2,1,0:T(8,128)(2,1)} %bitcast.23) | data formatting | bytes 16777216
  598.9 11.7 %copy.21 = f32[8,128,4096]{2,1,0:T(8,128)} copy(f32[8,128,4096]{2,1,0:T(8,128)} %bitcast.16) | data formatting | bytes 33554432
  (8 shorter events, 0.2 us)
Async XLA Ops:
  12.7 18.3 %copy-start = (bf16[4096,128]{1,0:T(8,128)(2,1)S(1)}, bf16[4096,128]{1,0:T(8,128)(2,1)}, u32[]{:S(2)}) copy-start(bf16[4096,128]{1,0:T(8,128)(2,1)} %wk_ref.1) | copy-start | bytes 3145732
  18.4 96.0 %collective-permute-start.2 = (bf16[512,2048]{1,0:T(8,128)(2,1)}, bf16[512,2048]{1,0:T(8,128)(2,1)}, u32[]{:S(2)}, u32[]{:S(2)}) collective-permute-start(bf16[512,2048]{1,0:T(8,128)(2,1)} %get-tuple-element.28), channel_id=1, source_target_pairs={{24,8},{0,16},{25,9},{1,17},{26,10},{2,18},{27,11},{3,19},{28,12},... | collective-permute-start | bytes 6291464 | tf_op jit(solution)/shard_map/ppermute | solution.py:739
  25.7 88.7 %collective-permute-start.1 = (bf16[512,2048]{1,0:T(8,128)(2,1)}, bf16[512,2048]{1,0:T(8,128)(2,1)}, u32[]{:S(2)}, u32[]{:S(2)}) collective-permute-start(bf16[512,2048]{1,0:T(8,128)(2,1)} %get-tuple-element.28), channel_id=1, source_target_pairs={{16,8},{8,16},{17,9},{9,17},{18,10},{10,18},{19,11},{11,19},{20,12... | collective-permute-start | bytes 6291464 | tf_op jit(solution)/shard_map/ppermute | solution.py:738
  27.6 86.7 %collective-permute-start = (bf16[512,2048]{1,0:T(8,128)(2,1)}, bf16[512,2048]{1,0:T(8,128)(2,1)}, u32[]{:S(2)}, u32[]{:S(2)}) collective-permute-start(bf16[512,2048]{1,0:T(8,128)(2,1)} %get-tuple-element.29), channel_id=1, source_target_pairs={{0,8},{24,16},{1,9},{25,17},{2,10},{26,18},{3,11},{27,19},{4,12},{... | collective-permute-start | bytes 6291464 | tf_op jit(solution)/shard_map/ppermute | solution.py:737

commit v2 on v1

--- a/solution.py
+++ b/solution.py
@@ -7,7 +7,7 @@
 from jax.sharding import PartitionSpec as P
 
 ROWS, DEPTH, LANE, TILE, BRICK, HALF_W = 1024, 4096, 128, 256, 512, 2048
-CHIPS, HEADS = 4, 8
+CHIPS, HEADS, GROUPS = 4, 8, 8
 VMEM_CAP = 66_000_000
 MESH = pl.DeviceIdType.MESH
 F32, BF16 = jnp.float32, jnp.bfloat16
@@ -23,6 +23,22 @@
     return lax.dot_general(lhs, rhs, dims, preferred_element_type=F32)
 
 
+def cost(gigaflops):
+    return pl.CostEstimate(flops=gigaflops * 10 ** 9, bytes_accessed=10 ** 8, transcendentals=0)
+
+
+def talking(collective_id):
+    return pltpu.CompilerParams(collective_id=collective_id, has_side_effects=True, vmem_limit_bytes=VMEM_CAP)
+
+
+def by_row(reduce, tile):
+    return reduce(tile, axis=1, keepdims=True)
+
+
+def twice(tile):
+    return jnp.concatenate([tile, tile], axis=0)
+
+
 def win(index, size):
     start = index * size
     return pl.ds(start if isinstance(start, int) else pl.multiple_of(start, size), size)
@@ -48,7 +64,7 @@
                 load_sem, wkv_sem, osem, send_sem, recv_sem):
     tp, cp = lax.axis_index("tp"), lax.axis_index("cp")
     peers = plane_peers(cp)
-    others, partner = peers[:-1], peers[-1]
+    *others, partner = peers
     barrier = pltpu.get_barrier_semaphore()
     for peer in peers:
         pl.semaphore_signal(barrier, inc=1, device_id=(tp, peer), device_id_type=MESH)
@@ -63,27 +79,34 @@
         copy.wait()
     for copy in loads_wq:
         copy.start()
-    sends = []
+    cos, sin = twice(cos_ref[...]), twice(sin_ref[...])
+    sends, stored = [], []
+
+    def share(i):
+        piece = kv_out.at[cp, rows[i]]
+        stored[i].wait()
+        sends.append([hand_over(piece, piece, send_sem.at[n, i], recv_sem.at[n, i], tp, peer) for n, peer in enumerate(peers)])
+        for copy in sends[i]:
+            copy.start()
+
     for i, row in enumerate(rows):
         if i:
             loads_h[i].wait()
         kv = dot(hbuf[row, :], wkvbuf[...])
-        kvbuf[row, win(0, LANE)] = rope(kv[:, :LANE], cos_ref[...], sin_ref[...])[0].astype(BF16)
+        kvbuf[row, win(0, LANE)] = rope(kv[:, :LANE], cos, sin)[0].astype(BF16)
         kvbuf[row, win(1, LANE)] = kv[:, LANE:].astype(BF16)
-        piece = kv_out.at[cp, row]
-        own = pltpu.make_async_copy(kvbuf.at[row], piece, osem.at[2 + i])
-        own.start()
+        stored.append(pltpu.make_async_copy(kvbuf.at[row], kv_out.at[cp, row], osem.at[2 + i]))
+        stored[i].start()
         if i == 0:
             pl.semaphore_wait(barrier, len(peers))
-        own.wait()
-        sends.append([hand_over(piece, piece, send_sem.at[n, i], recv_sem.at[n, i], tp, peer) for n, peer in enumerate(peers)])
-        for copy in sends[i]:
-            copy.start()
+        else:
+            share(i - 1)
+    share(CHIPS - 1)
     for copy in loads_wq:
         copy.wait()
     for copy in loads_g + loads_wo:
         copy.start()
-    cos2, sin2 = [jnp.concatenate([tab[...]] * 2, axis=0) for tab in (cos_ref, sin_ref)]
+    cos2, sin2 = twice(cos), twice(sin)
 
     @pl.loop(0, HEADS)
     def _(step):
@@ -126,6 +149,23 @@
     store_do.wait()
 
 
+def turn_kernel(w_ref, out_ref):
+    out_ref[...] = w_ref[...].reshape(BRICK, ROWS).T
+
+
+def turn(w):
+    return pl.pallas_call(
+        turn_kernel,
+        name="turn",
+        grid=(GROUPS,),
+        out_shape=jax.ShapeDtypeStruct((ROWS, DEPTH), BF16),
+        in_specs=[pl.BlockSpec((BRICK, HEADS, LANE), lambda i: (i, 0, 0))],
+        out_specs=pl.BlockSpec((ROWS, BRICK), lambda i: (0, i)),
+        compiler_params=pltpu.CompilerParams(vmem_limit_bytes=VMEM_CAP),
+        cost_estimate=cost(1),
+    )(w)
+
+
 def projections(h, g, wq_t, wo2, wk, wv, cos_tab, sin_tab, q_scale):
     square = (ROWS, ROWS)
     kv_shape = (HEADS, ROWS, TILE)
@@ -137,28 +177,29 @@
         out_specs=[ANY] * 3,
         scratch_shapes=[pltpu.VMEM(s, BF16) for s in [(ROWS, DEPTH)] * 4 + [(DEPTH, TILE), square, square, (ROWS, TILE)]]
         + [DMA(s) for s in ((CHIPS, CHIPS), (2,), (6,), (7, CHIPS), (7, CHIPS))],
-        compiler_params=pltpu.CompilerParams(collective_id=0, has_side_effects=True, vmem_limit_bytes=VMEM_CAP),
-        cost_estimate=pl.CostEstimate(flops=20_000_000_000, bytes_accessed=40_000_000, transcendentals=0),
+        compiler_params=talking(0),
+        cost_estimate=cost(20),
     )(h, g, wq_t, wo2, wk, wv, cos_tab, sin_tab)
 
 
 def attn_kernel(q_scale, q_ref, do_ref, kv_ref, mask_ref, cos_ref, sin_ref, o_ref, dq_ref, dkv_ref):
     keys = kv_ref[:, :, :LANE].reshape(ROWS, LANE)
     vals = kv_ref[:, :, LANE:].reshape(ROWS, LANE)
+    cos, sin, mask = twice(cos_ref[...]), twice(sin_ref[...]), twice(mask_ref[...])
     sums = []
     for pair in range(CHIPS):
         cols = [win(2 * pair + i, LANE) for i in range(2)]
         q = jnp.concatenate([q_ref[:, c] for c in cols], axis=0)
         do = jnp.concatenate([do_ref[:, c] for c in cols], axis=0)
-        scores = dot(q, keys, NT) + mask_ref[...]
-        prob = jnp.exp(scores - jnp.max(scores, axis=1, keepdims=True))
-        prob = prob * (1.0 / jnp.sum(prob, axis=1, keepdims=True))
+        scores = dot(q, keys, NT) + mask
+        prob = jnp.exp(scores - by_row(jnp.max, scores))
+        prob = prob * (1.0 / by_row(jnp.sum, prob))
         prob_b = prob.astype(BF16)
         out = dot(prob_b, vals).astype(BF16)
-        delta = jnp.sum(do.astype(F32) * out.astype(F32), axis=1, keepdims=True)
+        delta = by_row(jnp.sum, do.astype(F32) * out.astype(F32))
         d_score = (prob * (dot(do, vals, NT) - delta)).astype(BF16)
         dq = dot(d_score, keys)
-        dq = ((dq * cos_ref[...] - pltpu.roll(dq, LANE // 2, 1) * sin_ref[...]) * q_scale).astype(BF16)
+        dq = ((dq * cos - pltpu.roll(dq, LANE // 2, 1) * sin) * q_scale).astype(BF16)
         for i, c in enumerate(cols):
             o_ref[:, c] = out[i * LANE:(i + 1) * LANE]
             dq_ref[:, c] = dq[i * LANE:(i + 1) * LANE]
@@ -169,7 +210,7 @@
             dkv_ref[j, kind] = total[:, j * LANE:(j + 1) * LANE]
 
 
-def attention(q, do, kv, mask2, cos_tab, sin_tab, q_scale):
+def attention(q, do, kv, mask, cos_tab, sin_tab, q_scale):
     row_block = pl.BlockSpec((LANE, ROWS), lambda b: (b, 0))
     whole = lambda a: pl.BlockSpec(a.shape, lambda b: (0,) * a.ndim)
     return pl.pallas_call(
@@ -177,11 +218,11 @@
         name="attention",
         grid=(HEADS,),
         out_shape=[jax.ShapeDtypeStruct((ROWS, ROWS), BF16)] * 2 + [jax.ShapeDtypeStruct((HEADS, 2, TILE, BRICK), F32)],
-        in_specs=[row_block, row_block, pl.BlockSpec((HEADS, LANE, TILE), lambda b: (0, b, 0)), whole(mask2), whole(cos_tab), whole(sin_tab)],
+        in_specs=[row_block, row_block, pl.BlockSpec((HEADS, LANE, TILE), lambda b: (0, b, 0)), whole(mask), whole(cos_tab), whole(sin_tab)],
         out_specs=[row_block, row_block, pl.BlockSpec((HEADS, 2, LANE, LANE), lambda b: (0, 0, lax.div(b, CHIPS), lax.rem(b, CHIPS)))],
         compiler_params=pltpu.CompilerParams(vmem_limit_bytes=VMEM_CAP),
-        cost_estimate=pl.CostEstimate(flops=30_000_000_000, bytes_accessed=20_000_000, transcendentals=8_000_000),
-    )(q, do, kv, mask2, cos_tab, sin_tab)
+        cost_estimate=cost(30),
+    )(q, do, kv, mask, cos_tab, sin_tab)
 
 
 def tables(cp):
@@ -190,20 +231,19 @@
     inv_freq = 1.0 / jnp.power(10000.0, jnp.arange(half, dtype=F32) * (2.0 / LANE))
     ang = pos.astype(F32)[:, None] * inv_freq[None, :]
     cos, sin = jnp.cos(ang), jnp.sin(ang)
-    double = lambda tab: jnp.tile(tab, (2, 1))
     mask = jnp.where(jnp.arange(ROWS)[None, :] <= pos[:, None], 0.0, -jnp.inf).astype(F32)
-    return jnp.concatenate([cos.T, sin.T], axis=0), double(jnp.concatenate([cos, cos], axis=1)), double(jnp.concatenate([-sin, sin], axis=1)), double(mask)
+    return jnp.concatenate([cos.T, sin.T], axis=0), jnp.concatenate([cos, cos], axis=1), jnp.concatenate([-sin, sin], axis=1), mask
 
 
 DKV, DWO, DWQ, DWKV = 0, (1, 2), (3, 4), 5
-SETS, SLOTS, GROUPS = 6, 5, 8
+SETS, SLOTS = 6, 5
 LEADS, EARLY = (1, 3), 2
 FAR_ROLES = (0, 2, 3)
-INPUTS = ("o", "dq", "wo", "wq", "near", "mid", "far", "wkv", "g", "h", "dkv", "tabs")
+INPUTS = ("o", "dq", "wo", "wq", "near", "mid", "far", "wk", "wv", "g", "h", "dkv", "tabs")
 OUTPUTS = {"out": ((ROWS, DEPTH), BF16), "dh": ((ROWS, DEPTH), BF16), "dwo": ((ROWS, DEPTH), F32), "dwq": ((DEPTH, ROWS), F32),
            "dwkv": ((DEPTH, TILE), F32), "dkvb": ((ROWS, TILE), BF16), "wland": ((DEPTH, HALF_W), BF16),
            "pland": ((SETS, CHIPS, BRICK, BRICK), F32), "xland": ((SETS, 2, BRICK, BRICK), F32), "hland": ((SETS, 2, TILE, BRICK), F32), "zland": ((2, BRICK, BRICK), F32)}
-BUFFERS = {"abuf": ((ROWS, DEPTH + TILE), BF16), "wa": ((DEPTH + TILE, HALF_W), BF16), "wb": ((DEPTH + TILE, TILE), BF16),
+BUFFERS = {"abuf": ((ROWS, DEPTH + TILE), BF16), "wa": ((DEPTH, HALF_W), BF16), "wb": ((DEPTH, TILE), BF16), "wkv": ((DEPTH, TILE), BF16),
            "tile_a": ((LANE, HALF_W), BF16), "tile_b": ((ROWS, TILE), BF16), "keep": ((SLOTS, CHIPS, BRICK, BRICK), F32),
            "tmp": ((CHIPS, BRICK, BRICK), F32), "stage": ((2, BRICK, BRICK), F32), "left": ((2, ROWS, BRICK), BF16),
            "right": ((2, ROWS, BRICK), BF16), "zbuf": ((BRICK, BRICK), F32)}
@@ -263,8 +303,14 @@
         pl.semaphore_signal(self.credit.at[phase], inc=1, device_id=(self.plane(phase, 3), self.cp), device_id_type=MESH)
 
     def multiply(self, phase, kind, idx):
-        depth = pl.ds(0, DEPTH + TILE * phase)
-        act, weight = self.acts[phase], self.weights[phase]
+        weight = self.weights[phase]
+
+        def product(row, weights, col):
+            total = dot(self.abuf[row, pl.ds(0, DEPTH)], weights)
+            if phase:
+                total = total + dot(self.abuf[row, pl.ds(DEPTH, TILE)], self.wkv[col, :], NT)
+            return total.astype(BF16)
+
         if kind == 0:
             row = win(idx, LANE)
             for src in FAR_ROLES:
@@ -274,21 +320,19 @@
             @pl.loop(0, CHIPS)
             def _(i):
                 col = win(i, BRICK)
-                self.tile_a[:, col] = dot(self.abuf[row, depth], self.wa[depth, col]).astype(BF16)
+                self.tile_a[:, col] = product(row, self.wa[:, col], col)
         else:
             for src in FAR_ROLES:
                 self.cross_copy(phase, src, idx, 1 - self.core).wait_recv()
                 self.cross_copy(phase, src, idx, self.core).wait_send()
             pairs = [(self.wland.at[win(src, ROWS), win(idx, TILE)], self.wb.at[win(src, ROWS)]) for src in FAR_ROLES]
             pairs.append((weight.at[:, win(GROUPS + idx, TILE)], self.wb.at[win(1, ROWS)]))
-            if phase:
-                pairs.append((self.wkv.at[:, win(GROUPS + idx, TILE)], self.wb.at[pl.ds(DEPTH, TILE)]))
             self.move(pairs)
 
             @pl.loop(0, CHIPS)
             def _(i):
                 row = win(i, TILE)
-                self.tile_b[row, :] = dot(self.abuf[row, depth], self.wb[depth, :]).astype(BF16)
+                self.tile_b[row, :] = product(row, self.wb[...], win(GROUPS + idx, TILE))
 
         self.move([(self.tile_b if kind else self.tile_a, self.piece(phase, kind, idx))])
         for way, to_role in enumerate((0, 2)):
@@ -354,7 +398,7 @@
                 pairs = [(half, self.wa.at[win(2 * src + self.core, BRICK)]) for half, src in zip((self.near, self.mid, self.far), FAR_ROLES)]
                 pairs.append((self.weights[phase].at[:, win(0, HALF_W)], self.wa.at[win(1, ROWS)]))
                 pairs.append((self.acts[phase], self.abuf.at[:, win(1, ROWS)]))
-                pairs.append((self.wkv.at[:, win(0, HALF_W)], self.wa.at[pl.ds(DEPTH, TILE)]))
+                pairs += [(src, self.wkv.at[:, win(i, LANE)]) for i, src in enumerate((self.wk, self.wv))]
                 self.move(pairs)
 
     def end_swap(self):
@@ -632,8 +676,8 @@
 
 
 STEPS = {"add_pair": ((1, 3, 5, 7, 9, 22), (1, 5, 9, 13, 17, 23)), "relay": ((3, 6, 7, 10, 13, 24), (4, 8, 12, 16, 20, 25)),
-         "add_chips": ((6, 10, 13, 15, 18, 26), (7, 11, 15, 19, 23, 28)), "pass_on": ((0, 25, 26, 27, 28, 29), (0, 15, 19, 23, 27, 30)),
-         "pass_diagonal": ((0, 28, 29, 30, 31, 31), (0, 19, 23, 27, 31, 31))}
+         "add_chips": ((6, 10, 13, 15, 18, 26), (7, 11, 15, 19, 23, 28)), "pass_on": ((25, 26, 27, 28, 29), (15, 19, 23, 27, 30)),
+         "pass_diagonal": ((28, 29, 30, 31, 31), (19, 23, 27, 31, 31))}
 ONCE = {"hand_dkv": 0, "meet": 10, "settle": 15, "get_result": 17}
 PARTS, LATE = 16, 18
 
@@ -685,11 +729,10 @@
                 getattr(dev, step)()
 
         for step, (early, late) in STEPS.items():
-            for which in range(SETS):
-                if late[which]:
-                    @pl.when(now == jnp.where(busy, early[which], late[which]))
-                    def _():
-                        getattr(dev, step)(which)
+            for which in range(SETS - len(late), SETS):
+                @pl.when(now == jnp.where(busy, early[which - SETS], late[which - SETS]))
+                def _():
+                    getattr(dev, step)(which)
 
         @pl.loop(jnp.where(busy, jnp.maximum(2 * now - 2, 0), jnp.maximum(now - 1, 0)), jnp.minimum(jnp.where(busy, 2 * now, now), PARTS))
         def _(part):
@@ -718,9 +761,34 @@
         in_specs=[ANY] * len(operands),
         out_specs=[ANY] * len(OUTPUTS),
         scratch_shapes=[pltpu.VMEM(*spec) for spec in BUFFERS.values()] + [DMA(shape) for shape in SEMS.values()] + [pltpu.SemaphoreType.REGULAR((2,))],
-        compiler_params=pltpu.CompilerParams(collective_id=1, has_side_effects=True, vmem_limit_bytes=VMEM_CAP),
-        cost_estimate=pl.CostEstimate(flops=300_000_000_000, bytes_accessed=200_000_000, transcendentals=0),
+        compiler_params=talking(1),
+        cost_estimate=cost(300),
     )(*operands)
+
+
+def finish_kernel(out_ref, dh_ref, dwo_ref, dwq_ref, dwkv_ref, out, dh, dwo, dwq, dwk, dwv):
+    out[...] = out_ref[...]
+    dh[...] = dh_ref[...]
+    dwo[...] = dwo_ref[...]
+    dwq[...] = dwq_ref[...].reshape(dwq.shape)
+    dwk[...] = dwkv_ref[:, :LANE]
+    dwv[...] = dwkv_ref[:, LANE:]
+
+
+def finish(*arrays, steps=HEADS):
+    heads = (DEPTH, HEADS, LANE)
+    shapes = [(arrays[0].shape, BF16), (arrays[1].shape, BF16), (arrays[2].shape, F32), (heads, F32), ((DEPTH, LANE), F32), ((DEPTH, LANE), F32)]
+    block = lambda shape: pl.BlockSpec((shape[0] // steps, *shape[1:]), lambda i: (i,) + (0,) * (len(shape) - 1))
+    return pl.pallas_call(
+        finish_kernel,
+        name="finish",
+        grid=(steps,),
+        out_shape=[jax.ShapeDtypeStruct(*spec) for spec in shapes],
+        in_specs=[block(a.shape) for a in arrays],
+        out_specs=[block(shape) for shape, _ in shapes],
+        compiler_params=pltpu.CompilerParams(vmem_limit_bytes=VMEM_CAP),
+        cost_estimate=cost(1),
+    )(*arrays)
 
 
 def solution(mesh):
@@ -728,20 +796,18 @@
         tp, cp = lax.axis_index("tp"), lax.axis_index("cp")
         h, g = hidden.reshape(ROWS, DEPTH), grad_out.reshape(ROWS, DEPTH)
         q_scale = LANE ** -0.5
-        tabs, cos_tab, sin_tab, mask2 = tables(cp)
+        tabs, cos_tab, sin_tab, mask = tables(cp)
         wo2 = w_out.reshape(ROWS, DEPTH)
-        wq_t = w_query.transpose(1, 2, 0).reshape(ROWS, DEPTH)
-        wkv_t = jnp.concatenate([w_key, w_value], axis=1).T
+        wq_t = turn(w_query)
         wo_half, wq_half = [lax.dynamic_slice(w, (lax.rem(cp, 2) * BRICK, 0), (BRICK, HALF_W)) for w in (wo2, wq_t)]
         one_way, other_way = jnp.where(tp <= 1, wo_half, wq_half), jnp.where(tp <= 1, wq_half, wo_half)
         near = lax.ppermute(one_way, "tp", [(0, 1), (3, 2)])
         mid = lax.ppermute(other_way, "tp", [(2, 1), (1, 2)])
         far = lax.ppermute(other_way, "tp", [(3, 1), (0, 2)])
         q, d_o, kv = projections(h, g, wq_t, wo2, w_key, w_value, cos_tab, sin_tab, q_scale)
-        o, dq, dkv = attention(q, d_o, kv, mask2, cos_tab, sin_tab, q_scale)
-        out, dh, dwo, dwq, dwkv = exchange(o, dq, wo2, wq_t, near, mid, far, wkv_t, g, h, dkv.reshape(HEADS, BRICK, BRICK), tabs)[:5]
-        return (out.reshape(hidden.shape), dh.reshape(hidden.shape), dwq.reshape(w_query.shape),
-                dwkv[:, :LANE], dwkv[:, LANE:], dwo.reshape(w_out.shape))
+        o, dq, dkv = attention(q, d_o, kv, mask, cos_tab, sin_tab, q_scale)
+        out, dh, dwo, dwq, dwk, dwv = finish(*exchange(o, dq, wo2, wq_t, near, mid, far, w_key, w_value, g, h, dkv.reshape(HEADS, BRICK, BRICK), tabs)[:5])
+        return out.reshape(hidden.shape), dh.reshape(hidden.shape), dwq, dwk, dwv, dwo.reshape(w_out.shape)
 
     row_spec, head_spec = P(None, "cp", None), P("tp", None, None)
     query_spec = P(None, "tp", None)

time: 612 us -> 598 us (0.977)
  local copies, waits for them, and re-layouts: 62.7 us -> 0 us
  Pallas kernels: 524 us -> 566 us
    pallas_call x0 -> x2, Pallas kernels: none -> 44.4 us  [the longest x1 34.6 us: finish(): pl.pallas_call(finish_kernel, name='finish', grid=(steps,), out_shape=[ja...]
    unnamed x8 -> x0, local copies, waits for them, and re-layouts: 43.7 us -> none
    transpose x1 -> x0, local copies, waits for them, and re-layouts: 12.1 us -> none  [local_program(): wq_t = w_query.transpose(1, 2, 0).reshape(ROWS, DEPTH)]
where the time goes in v2:
time: 598 us; the launch traced here: 597 us
  Pallas kernels  566 us (95%)
  starting transfers between devices  11.9 us (2%)
  other arithmetic  9.11 us (2%)
  waiting for transfers between devices  8.71 us (1%)
    pallas_call x1, Pallas kernels, exchange(): pl.pallas_call(exchange_kernel, name='exchange', out_shape=[jax.ShapeDtyp...  450 us
    pallas_call x1, Pallas kernels, attention(): pl.pallas_call(functools.partial(attn_kernel, q_scale), name='attention',...  37.4 us
    pallas_call x1, Pallas kernels, finish(): pl.pallas_call(finish_kernel, name='finish', grid=(steps,), out_shape=[ja...  34.6 us
    pallas_call x1, Pallas kernels, projections(): pl.pallas_call(functools.partial(proj_kernel, q_scale), name='projections...  34.5 us
  transfers between devices with their start and end apart: 3, of which 1 were waited for; matrix products, arithmetic and copies ran while one was open for 1% of the time, Pallas kernels for 12%

profile of v2, /device:TPU:0, one launch (start us, length us, event | category | flops | bytes accessed | tf_op | source)
XLA Modules:
  0.0 596.8 jit_solution(15623221859118992839)
XLA Ops:
  0.6 9.9 %turn.1.wq_ref.refs_3_ = bf16[1024,4096]{1,0:T(8,128)(2,1)} custom-call(bf16[4096,8,128]{2,1,0:T(8,128)(2,1)} %w_ref.1), custom_call_target="tpu_custom_call" | custom-call | flops 1000000000 | bytes 100000000 | tf_op jit(solution)/shard_map/turn/pallas_call | solution.py:157
  10.5 5.6 broadcast_select_fusion
  16.1 7.3 %collective-permute-start.2 = (bf16[512,2048]{1,0:T(8,128)(2,1)}, bf16[512,2048]{1,0:T(8,128)(2,1)}, u32[]{:S(2)}, u32[]{:S(2)}) collective-permute-start(bf16[512,2048]{1,0:T(8,128)(2,1)} %get-tuple-element.40), channel_id=1, source_target_pairs={{24,8},{0,16},{25,9},{1,17},{26,10},{2,18},{27,11},{3,19},{28,12},... | collective-permute-start | bytes 6291464 | tf_op jit(solution)/shard_map/ppermute | solution.py:806
  23.4 2.0 collective-permute-start.1
  25.4 2.6 collective-permute-start
  28.0 0.2 multiply_cosine_fusion.1
  28.2 0.3 fusion.1
  28.5 0.7 pad_maximum_fusion.cos_ref
  29.2 0.9 fusion.mask_ref
  30.1 0.6 pad_maximum_fusion.2.refs_12_
  30.8 0.7 pad_maximum_fusion.1.sin_ref
  31.5 34.5 %projections.1 = (bf16[1024,1024]{1,0:T(8,128)(2,1)}, bf16[1024,1024]{1,0:T(8,128)(2,1)}, bf16[8,1024,256]{2,1,0:T(8,128)(2,1)}) custom-call(bf16[1024,4096]{1,0:T(8,128)(2,1)} %bitcast.11, bf16[1024,4096]{1,0:T(8,128)(2,1)} %bitcast.13, bf16[1024,4096]{1,0:T(8,128)(2,1)} %turn.1.wq_ref.refs_3_, bf16[1024,4096]{1,0:T(8,128)(2,1)} %bitcast.8, ...), custom_call_target="tpu_custom_call" | custom-call | flops 20000000000 | bytes 100000000 | tf_op jit(solution)/shard_map/projections/pallas_call | solution.py:172
  66.0 37.4 %attention.1 = (bf16[1024,1024]{1,0:T(8,128)(2,1)}, bf16[1024,1024]{1,0:T(8,128)(2,1)}, f32[8,2,256,512]{3,2,1,0:T(8,128)}) custom-call(bf16[1024,1024]{1,0:T(8,128)(2,1)} %get-tuple-element.23.q_ref, bf16[1024,1024]{1,0:T(8,128)(2,1)} %get-tuple-element.24.do_ref, bf16[8,1024,256]{2,1,0:T(8,128)(2,1)} %get-tuple-element.25.kv_ref, ...), custom_call_target="tpu_custom_call" | custom-call | flops 30000001024 | bytes 100000000 | tf_op jit(solution)/shard_map/attention/pallas_call | solution.py:216
  103.3 8.7 %collective-permute-done.refs_4_ = bf16[512,2048]{1,0:T(8,128)(2,1)} collective-permute-done((bf16[512,2048]{1,0:T(8,128)(2,1)}, bf16[512,2048]{1,0:T(8,128)(2,1)}, u32[]{:S(2)}, u32[]{:S(2)}) %collective-permute-start) | collective-permute-done | bytes 2097184 | tf_op jit(solution)/shard_map/ppermute | solution.py:804
  112.0 0.0 collective-permute-done.2.refs_6_
  112.0 0.0 collective-permute-done.1.refs_5_
  112.0 450.1 %exchange.1 = (bf16[1024,4096]{1,0:T(8,128)(2,1)}, bf16[1024,4096]{1,0:T(8,128)(2,1)}, f32[1024,4096]{1,0:T(8,128)}, f32[4096,1024]{1,0:T(8,128)}, f32[4096,256]...) custom-call(bf16[1024,1024]{1,0:T(8,128)(2,1)} %get-tuple-element.26, ...), custom_call_target="tpu_custom_call" | custom-call | flops 299999985664 | bytes 100000000 | tf_op jit(solution)/shard_map/exchange/pallas_call | solution.py:757
  562.2 34.6 %finish.1 = (bf16[1024,4096]{1,0:T(8,128)(2,1)}, bf16[1024,4096]{1,0:T(8,128)(2,1)}, f32[1024,4096]{1,0:T(8,128)}, f32[4096,8,128]{2,1,0:T(8,128)}, f32[4096,128]{1,0:T(8,128)}, /*index=5*/f32[4096,128]{1,0:T(8,128)}) custom-call(bf16[1024,4096]{1,0:T(8,128)(2,1)} %get-tuple-element.29.out_ref, bf16[1024,4096]{1,0:T(8,128)(2,1)} %get-tuple-element.30.dh_ref, ...), custom_call_target="tpu_custom_call" | custom-call | flops 1000000000 | bytes 100000000 | tf_op jit(solution)/shard_map/finish/pallas_call | solution.py:782
  (2 shorter events, 0.0 us)
Async XLA Ops:
  16.1 96.0 %collective-permute-start.2 = (bf16[512,2048]{1,0:T(8,128)(2,1)}, bf16[512,2048]{1,0:T(8,128)(2,1)}, u32[]{:S(2)}, u32[]{:S(2)}) collective-permute-start(bf16[512,2048]{1,0:T(8,128)(2,1)} %get-tuple-element.40), channel_id=1, source_target_pairs={{24,8},{0,16},{25,9},{1,17},{26,10},{2,18},{27,11},{3,19},{28,12},... | collective-permute-start | bytes 6291464 | tf_op jit(solution)/shard_map/ppermute | solution.py:806
  23.4 88.7 %collective-permute-start.1 = (bf16[512,2048]{1,0:T(8,128)(2,1)}, bf16[512,2048]{1,0:T(8,128)(2,1)}, u32[]{:S(2)}, u32[]{:S(2)}) collective-permute-start(bf16[512,2048]{1,0:T(8,128)(2,1)} %get-tuple-element.40), channel_id=1, source_target_pairs={{16,8},{8,16},{17,9},{9,17},{18,10},{10,18},{19,11},{11,19},{20,12... | collective-permute-start | bytes 6291464 | tf_op jit(solution)/shard_map/ppermute | solution.py:805
  25.4 86.7 %collective-permute-start = (bf16[512,2048]{1,0:T(8,128)(2,1)}, bf16[512,2048]{1,0:T(8,128)(2,1)}, u32[]{:S(2)}, u32[]{:S(2)}) collective-permute-start(bf16[512,2048]{1,0:T(8,128)(2,1)} %get-tuple-element.41), channel_id=1, source_target_pairs={{0,8},{24,16},{1,9},{25,17},{2,10},{26,18},{3,11},{27,19},{4,12},{... | collective-permute-start | bytes 6291464 | tf_op jit(solution)/shard_map/ppermute | solution.py:804

commit v3 on v2

--- a/solution.py
+++ b/solution.py
@@ -237,19 +237,21 @@
 
 DKV, DWO, DWQ, DWKV = 0, (1, 2), (3, 4), 5
 SETS, SLOTS = 6, 5
-LEADS, EARLY = (1, 3), 2
+LEADS, EARLY = (3, 2), 3
+LATER = (5, 6, 7, )
 FAR_ROLES = (0, 2, 3)
+PHASES, SOURCES = 2, len(FAR_ROLES)
 INPUTS = ("o", "dq", "wo", "wq", "near", "mid", "far", "wk", "wv", "g", "h", "dkv", "tabs")
 OUTPUTS = {"out": ((ROWS, DEPTH), BF16), "dh": ((ROWS, DEPTH), BF16), "dwo": ((ROWS, DEPTH), F32), "dwq": ((DEPTH, ROWS), F32),
            "dwkv": ((DEPTH, TILE), F32), "dkvb": ((ROWS, TILE), BF16), "wland": ((DEPTH, HALF_W), BF16),
-           "pland": ((SETS, CHIPS, BRICK, BRICK), F32), "xland": ((SETS, 2, BRICK, BRICK), F32), "hland": ((SETS, 2, TILE, BRICK), F32), "zland": ((2, BRICK, BRICK), F32)}
+           "pland": ((SETS, CHIPS, BRICK, BRICK), F32), "xland": ((SETS, PHASES, BRICK, BRICK), F32), "hland": ((SETS, PHASES, TILE, BRICK), F32), "zland": ((PHASES, BRICK, BRICK), F32)}
 BUFFERS = {"abuf": ((ROWS, DEPTH + TILE), BF16), "wa": ((DEPTH, HALF_W), BF16), "wb": ((DEPTH, TILE), BF16), "wkv": ((DEPTH, TILE), BF16),
            "tile_a": ((LANE, HALF_W), BF16), "tile_b": ((ROWS, TILE), BF16), "keep": ((SLOTS, CHIPS, BRICK, BRICK), F32),
-           "tmp": ((CHIPS, BRICK, BRICK), F32), "stage": ((2, BRICK, BRICK), F32), "left": ((2, ROWS, BRICK), BF16),
-           "right": ((2, ROWS, BRICK), BF16), "zbuf": ((BRICK, BRICK), F32)}
-SEMS = {"load": (12,), "early": (4,), "asend": (2, GROUPS), "arecv": (2, 3, GROUPS), "wsend": (2, GROUPS), "wrecv": (2, 3, GROUPS), "fsend": (2, 3), "frecv": (2, 3, GROUPS),
-        "rsend": (2, 2, 2, GROUPS), "rrecv": (2, 2, GROUPS), "swsend": (3,), "swrecv": (3,), "dsend": (SETS, CHIPS), "drecv": (SETS, CHIPS),
-        "xsend": (SETS, 2), "xrecv": (SETS, 2), "hsend": (SETS, 2), "hrecv": (SETS, 2), "zsend": (3,), "zrecv": (3,), "gsend": (SETS, 9), "grecv": (SETS, 9)}
+           "tmp": ((CHIPS, BRICK, BRICK), F32), "stage": ((PHASES, BRICK, BRICK), F32), "left": ((PHASES, ROWS, BRICK), BF16),
+           "right": ((PHASES, ROWS, BRICK), BF16), "zbuf": ((BRICK, BRICK), F32)}
+SEMS = {"load": (12,), "early": (CHIPS,), "held": (CHIPS,), "asend": (PHASES, GROUPS), "arecv": (PHASES, SOURCES, GROUPS), "wsend": (PHASES, GROUPS), "wrecv": (PHASES, SOURCES, GROUPS), "fsend": (PHASES, SOURCES), "frecv": (PHASES, SOURCES, GROUPS),
+        "rsend": (PHASES, PHASES, PHASES, GROUPS), "rrecv": (PHASES, PHASES, GROUPS), "swsend": (SOURCES,), "swrecv": (SOURCES,), "dsend": (SETS, CHIPS), "drecv": (SETS, CHIPS),
+        "xsend": (SETS, PHASES), "xrecv": (SETS, PHASES), "hsend": (SETS, PHASES), "hrecv": (SETS, PHASES), "zsend": (SOURCES,), "zrecv": (SOURCES,), "gsend": (SETS, 9), "grecv": (SETS, 9)}
 
 
 class Exchange:
@@ -388,7 +390,7 @@
                 self.w_copy(phase, src, n, self.plane(phase, 1)).start()
 
     def start_line(self):
-        for phase in range(2):
+        for phase in range(PHASES):
             @pl.when(self.role(phase) == 1)
             def _():
                 swaps = []
@@ -408,9 +410,9 @@
                 hand_over(half, self.wa.at[win(2 * src + 1 - self.core, BRICK)], self.swsend.at[i], self.swrecv.at[i], self.tp, self.partner).wait()
 
     def end_line(self):
-        for phase in range(2):
+        for phase in range(PHASES):
             role = self.role(phase)
-            for kind in range(2):
+            for kind in range(PHASES):
                 @pl.when(role == 1)
                 def _():
                     @pl.loop(0, GROUPS)
@@ -455,13 +457,14 @@
                           self.hsend.at[which, n], self.hrecv.at[which, n], self.tp, peer) for n, peer in enumerate((self.x, self.y))]
 
     def own_blocks(self):
-        return [pltpu.make_async_copy(self.dkv.at[2 * i + self.core], self.keep.at[0, i], self.early.at[i]) for i in range(CHIPS)]
+        return [pltpu.make_async_copy(self.dkv.at[2 * i + self.core], self.keep.at[0, i], self.held.at[i]) for i in range(CHIPS)]
 
     def hand_dkv(self):
         for i in range(CHIPS):
             self.pair_copy(DKV, i, self.dkv.at[2 * i + 1 - self.core]).start()
         for copy in self.own_blocks():
             copy.start()
+        self.fetch(0)
 
     def fetch(self, part):
         half, i = win(lax.rem(lax.div(part, CHIPS), 2), BRICK), lax.rem(part, CHIPS)
@@ -483,9 +486,15 @@
         col = pl.ds(0, BRICK if kind is None else TILE)
         slot = self.stage.at[lax.rem(part, 2), :, col]
 
-        @pl.when(i > 1)
-        def _():
-            self.pair_copy(kind, i - 2, slot, which).wait_send()
+        before = part - 2
+
+        @pl.when((before >= 0) & (before < PARTS))
+        def _():
+            self.pair_copy(None, lax.rem(before, CHIPS), self.stage.at[0], 1 + lax.div(before, CHIPS)).wait_send()
+
+        @pl.when(before >= PARTS)
+        def _():
+            self.pair_copy(DWKV, before - PARTS, self.brick(DWKV, self.stage.at[0])).wait_send()
 
         for n, dst in enumerate((slot, self.keep.at[lax.rem(which, SLOTS), i, :, col])):
             left, right = self.left.at[n], self.right.at[n, :, col]
@@ -509,12 +518,11 @@
         landed = [self.brick(which, self.pland.at[which, i]) for i in range(CHIPS)]
         for i in range(CHIPS):
             self.pair_copy(which, i, landed[i]).wait_recv()
-        for i in range(0 if which == DKV else CHIPS // 2, CHIPS):
+        for i in range({DKV: 0, DWKV: 2}.get(which, CHIPS), CHIPS):
             self.pair_copy(which, i, landed[i]).wait_send()
         if which == DKV:
             for copy in self.own_blocks():
                 copy.wait()
-            self.fetch(0)
         self.move([(landed[i], self.brick(which, self.tmp.at[i])) for i in range(CHIPS)])
         col = pl.ds(0, TILE if which == DWKV else BRICK)
 
@@ -585,7 +593,7 @@
             self.share_copy(which, kind).start()
 
     def pass_on(self, which):
-        for kind in range(2):
+        for kind in range(PHASES):
             self.shared_place(which, kind).wait_recv()
         for kind in (5, 6, 3, 4):
             self.share_copy(which, kind).start()
@@ -625,6 +633,7 @@
                 self.total(DKV, 1, add)
                 if inner == 2:
                     self.z_copy(1, 1).start()
+                    self.feed(0, 2, (), LATER)
 
     def settle(self):
         half = LANE // 2
@@ -635,7 +644,7 @@
             self.move([(self.zland.at[1], self.tmp.at[0]), (self.tabs, self.tmp.at[1, win(0, LANE), win(0, LANE)])])
             for b in range(HEADS):
                 cos, sin = self.tmp[1, win(0, half), win(0, LANE)], self.tmp[1, win(1, half), win(0, LANE)]
-                for kind in range(2):
+                for kind in range(PHASES):
                     row, col = win(2 * kind + b // CHIPS, LANE), win(b % CHIPS, LANE)
                     part = self.zbuf[row, col] + self.tmp[0, row, col]
                     if kind == 0:
@@ -672,14 +681,15 @@
         def _():
             self.z_result(2, 3).wait_send()
 
-        self.fetch(PARTS)
-
-
-STEPS = {"add_pair": ((1, 3, 5, 7, 9, 22), (1, 5, 9, 13, 17, 23)), "relay": ((3, 6, 7, 10, 13, 24), (4, 8, 12, 16, 20, 25)),
-         "add_chips": ((6, 10, 13, 15, 18, 26), (7, 11, 15, 19, 23, 28)), "pass_on": ((25, 26, 27, 28, 29), (15, 19, 23, 27, 30)),
-         "pass_diagonal": ((28, 29, 30, 31, 31), (19, 23, 27, 31, 31))}
-ONCE = {"hand_dkv": 0, "meet": 10, "settle": 15, "get_result": 17}
-PARTS, LATE = 16, 18
+
+STEPS = {"add_pair": ((1, 3, 5, 9, 9, 22), (2, 5, 5, 7, 11, 27)),
+         "relay": ((2, 5, 11, 12, 14, 26), (3, 9, 14, 11, 12, 28)),
+         "add_chips": ((9, 9, 14, 21, 23, 30), (6, 12, 21, 21, 16, 30)),
+         "pass_on": ((19, 25, 27, 26, 31), (17, 25, 29, 20, 31)),
+         "pass_diagonal": ((27, 28, 30, 31, 31), (21, 29, 31, 24, 31))}
+ONCE = {"hand_dkv": 0, "meet": 10, "get_result": 17}
+PARTS, LATE = 16, (18, 18)
+TURN, TURNS, NEAR, MID = 13, (13, 16, 13, 14), (10, 20), (16, 16)
 
 
 def exchange_kernel(*refs):
@@ -698,7 +708,7 @@
         if i <= LEADS[1]:
             dev.feed(1, 3, (i - 1,), ())
     dev.feed(0, 0, (), blocks)
-    dev.feed(0, 2, blocks, blocks)
+    dev.feed(0, 2, blocks, blocks[:GROUPS - len(LATER)])
     dev.feed(1, 2, blocks[:EARLY], ())
     dev.start_line()
     dev.end_swap()
@@ -706,13 +716,24 @@
 
     @pl.loop(0, CHIPS * GROUPS)
     def _(now):
-        idx = lax.rem(now, GROUPS)
-        spans = [(lax.div(now, GROUPS) == 2 * phase + kind, phase, kind) for phase in range(2) for kind in range(2)]
-
-        @pl.when(now == 2 * GROUPS)
-        def _():
-            dev.feed(1, 0, blocks, blocks)
-            dev.feed(1, 2, blocks[EARLY:], blocks)
+        turn = TURNS[0]
+        for plane, own_turn in enumerate(TURNS):
+            turn = jnp.where(dev.tp == plane, own_turn, turn)
+        ahead = now - turn
+        job = jnp.where(lax.rem(ahead, 2) == 0, 2 * GROUPS, turn) + lax.div(ahead, 2)
+        job = jnp.where((ahead >= 0) & (now + turn < CHIPS * GROUPS), job, now)
+        idx = lax.rem(job, GROUPS)
+        spans = [(lax.div(job, GROUPS) == 2 * phase + kind, phase, kind) for phase in range(PHASES) for kind in range(PHASES)]
+
+        for slots, src, acts in ((NEAR, 0, blocks), (MID, 2, blocks[EARLY:])):
+            for slot, operands in zip(slots, ((acts, ()), ((), blocks))):
+                @pl.when(now == slot)
+                def _():
+                    dev.feed(1, src, *operands)
+
+        @pl.when(now == TURN)
+        def _():
+            dev.settle()
             dev.take()
 
         for here, phase, kind in spans:
@@ -734,13 +755,19 @@
                 def _():
                     getattr(dev, step)(which)
 
-        @pl.loop(jnp.where(busy, jnp.maximum(2 * now - 2, 0), jnp.maximum(now - 1, 0)), jnp.minimum(jnp.where(busy, 2 * now, now), PARTS))
+        @pl.loop(jnp.clip(2 * now - 2, 0, PARTS), jnp.clip(2 * now, 0, PARTS))
         def _(part):
             dev.make(part)
 
-        @pl.when((now >= LATE) & (now < LATE + CHIPS))
-        def _():
-            dev.make(now + PARTS - LATE, DWKV)
+        late = now - jnp.where(busy, *LATE)
+
+        @pl.when(late == 0)
+        def _():
+            dev.fetch(PARTS)
+
+        @pl.when((late >= 0) & (late < CHIPS))
+        def _():
+            dev.make(late + PARTS, DWKV)
 
         for here, phase, kind in spans:
             if kind:

time: 598 us -> 581 us (0.972)
  Pallas kernels: 566 us -> 549 us
    pallas_call x1, Pallas kernels: 450 us -> 433 us  [exchange(): pl.pallas_call(exchange_kernel, name='exchange', out_shape=[jax.ShapeDtyp...]
where the time goes in v3:
time: 581 us; the launch traced here: 580 us
  Pallas kernels  549 us (94%)
  starting transfers between devices  11.9 us (2%)
  other arithmetic  9.11 us (2%)
  waiting for transfers between devices  8.71 us (1%)
    pallas_call x1, Pallas kernels, exchange(): pl.pallas_call(exchange_kernel, name='exchange', out_shape=[jax.ShapeDtyp...  433 us
    pallas_call x1, Pallas kernels, attention(): pl.pallas_call(functools.partial(attn_kernel, q_scale), name='attention',...  37.4 us
    pallas_call x1, Pallas kernels, finish(): pl.pallas_call(finish_kernel, name='finish', grid=(steps,), out_shape=[ja...  34.6 us
    pallas_call x1, Pallas kernels, projections(): pl.pallas_call(functools.partial(proj_kernel, q_scale), name='projections...  34.5 us
  transfers between devices with their start and end apart: 3, of which 1 were waited for; matrix products, arithmetic and copies ran while one was open for 1% of the time, Pallas kernels for 12%

profile of v3, /device:TPU:0, one launch (start us, length us, event | category | flops | bytes accessed | tf_op | source)
XLA Modules:
  0.0 579.6 jit_solution(7013455136493862098)
XLA Ops:
  0.6 9.9 %turn.1.wq_ref.refs_3_ = bf16[1024,4096]{1,0:T(8,128)(2,1)} custom-call(bf16[4096,8,128]{2,1,0:T(8,128)(2,1)} %w_ref.1), custom_call_target="tpu_custom_call" | custom-call | flops 1000000000 | bytes 100000000 | tf_op jit(solution)/shard_map/turn/pallas_call | solution.py:157
  10.5 5.6 broadcast_select_fusion
  16.1 7.3 %collective-permute-start.2 = (bf16[512,2048]{1,0:T(8,128)(2,1)}, bf16[512,2048]{1,0:T(8,128)(2,1)}, u32[]{:S(2)}, u32[]{:S(2)}) collective-permute-start(bf16[512,2048]{1,0:T(8,128)(2,1)} %get-tuple-element.40), channel_id=1, source_target_pairs={{24,8},{0,16},{25,9},{1,17},{26,10},{2,18},{27,11},{3,19},{28,12},... | collective-permute-start | bytes 6291464 | tf_op jit(solution)/shard_map/ppermute | solution.py:833
  23.4 2.0 collective-permute-start.1
  25.4 2.6 collective-permute-start
  28.0 0.2 multiply_cosine_fusion.1
  28.2 0.3 fusion.1
  28.5 0.7 pad_maximum_fusion.cos_ref
  29.2 0.9 fusion.mask_ref
  30.1 0.6 pad_maximum_fusion.2.refs_12_
  30.8 0.7 pad_maximum_fusion.1.sin_ref
  31.5 34.5 %projections.1 = (bf16[1024,1024]{1,0:T(8,128)(2,1)}, bf16[1024,1024]{1,0:T(8,128)(2,1)}, bf16[8,1024,256]{2,1,0:T(8,128)(2,1)}) custom-call(bf16[1024,4096]{1,0:T(8,128)(2,1)} %bitcast.11, bf16[1024,4096]{1,0:T(8,128)(2,1)} %bitcast.13, bf16[1024,4096]{1,0:T(8,128)(2,1)} %turn.1.wq_ref.refs_3_, bf16[1024,4096]{1,0:T(8,128)(2,1)} %bitcast.8, ...), custom_call_target="tpu_custom_call" | custom-call | flops 20000000000 | bytes 100000000 | tf_op jit(solution)/shard_map/projections/pallas_call | solution.py:172
  66.0 37.4 %attention.1 = (bf16[1024,1024]{1,0:T(8,128)(2,1)}, bf16[1024,1024]{1,0:T(8,128)(2,1)}, f32[8,2,256,512]{3,2,1,0:T(8,128)}) custom-call(bf16[1024,1024]{1,0:T(8,128)(2,1)} %get-tuple-element.23.q_ref, bf16[1024,1024]{1,0:T(8,128)(2,1)} %get-tuple-element.24.do_ref, bf16[8,1024,256]{2,1,0:T(8,128)(2,1)} %get-tuple-element.25.kv_ref, ...), custom_call_target="tpu_custom_call" | custom-call | flops 30000001024 | bytes 100000000 | tf_op jit(solution)/shard_map/attention/pallas_call | solution.py:216
  103.3 8.7 %collective-permute-done.refs_4_ = bf16[512,2048]{1,0:T(8,128)(2,1)} collective-permute-done((bf16[512,2048]{1,0:T(8,128)(2,1)}, bf16[512,2048]{1,0:T(8,128)(2,1)}, u32[]{:S(2)}, u32[]{:S(2)}) %collective-permute-start) | collective-permute-done | bytes 2097184 | tf_op jit(solution)/shard_map/ppermute | solution.py:831
  112.0 0.0 collective-permute-done.2.refs_6_
  112.0 0.0 collective-permute-done.1.refs_5_
  112.0 432.9 %exchange.1 = (bf16[1024,4096]{1,0:T(8,128)(2,1)}, bf16[1024,4096]{1,0:T(8,128)(2,1)}, f32[1024,4096]{1,0:T(8,128)}, f32[4096,1024]{1,0:T(8,128)}, f32[4096,256]...) custom-call(bf16[1024,1024]{1,0:T(8,128)(2,1)} %get-tuple-element.26, ...), custom_call_target="tpu_custom_call" | custom-call | flops 299999985664 | bytes 100000000 | tf_op jit(solution)/shard_map/exchange/pallas_call | solution.py:784
  545.0 34.6 %finish.1 = (bf16[1024,4096]{1,0:T(8,128)(2,1)}, bf16[1024,4096]{1,0:T(8,128)(2,1)}, f32[1024,4096]{1,0:T(8,128)}, f32[4096,8,128]{2,1,0:T(8,128)}, f32[4096,128]{1,0:T(8,128)}, /*index=5*/f32[4096,128]{1,0:T(8,128)}) custom-call(bf16[1024,4096]{1,0:T(8,128)(2,1)} %get-tuple-element.29.out_ref, bf16[1024,4096]{1,0:T(8,128)(2,1)} %get-tuple-element.30.dh_ref, ...), custom_call_target="tpu_custom_call" | custom-call | flops 1000000000 | bytes 100000000 | tf_op jit(solution)/shard_map/finish/pallas_call | solution.py:809
  (2 shorter events, 0.0 us)
Async XLA Ops:
  16.1 96.0 %collective-permute-start.2 = (bf16[512,2048]{1,0:T(8,128)(2,1)}, bf16[512,2048]{1,0:T(8,128)(2,1)}, u32[]{:S(2)}, u32[]{:S(2)}) collective-permute-start(bf16[512,2048]{1,0:T(8,128)(2,1)} %get-tuple-element.40), channel_id=1, source_target_pairs={{24,8},{0,16},{25,9},{1,17},{26,10},{2,18},{27,11},{3,19},{28,12},... | collective-permute-start | bytes 6291464 | tf_op jit(solution)/shard_map/ppermute | solution.py:833
  23.4 88.7 %collective-permute-start.1 = (bf16[512,2048]{1,0:T(8,128)(2,1)}, bf16[512,2048]{1,0:T(8,128)(2,1)}, u32[]{:S(2)}, u32[]{:S(2)}) collective-permute-start(bf16[512,2048]{1,0:T(8,128)(2,1)} %get-tuple-element.40), channel_id=1, source_target_pairs={{16,8},{8,16},{17,9},{9,17},{18,10},{10,18},{19,11},{11,19},{20,12... | collective-permute-start | bytes 6291464 | tf_op jit(solution)/shard_map/ppermute | solution.py:832
  25.4 86.7 %collective-permute-start = (bf16[512,2048]{1,0:T(8,128)(2,1)}, bf16[512,2048]{1,0:T(8,128)(2,1)}, u32[]{:S(2)}, u32[]{:S(2)}) collective-permute-start(bf16[512,2048]{1,0:T(8,128)(2,1)} %get-tuple-element.41), channel_id=1, source_target_pairs={{0,8},{24,16},{1,9},{25,17},{2,10},{26,18},{3,11},{27,19},{4,12},{... | collective-permute-start | bytes 6291464 | tf_op jit(solution)/shard_map/ppermute | solution.py:831

commit v4 on v3

--- a/solution.py
+++ b/solution.py
@@ -150,17 +150,17 @@
 
 
 def turn_kernel(w_ref, out_ref):
-    out_ref[...] = w_ref[...].reshape(BRICK, ROWS).T
+    out_ref[...] = w_ref[...].reshape(ROWS, ROWS).T
 
 
 def turn(w):
     return pl.pallas_call(
         turn_kernel,
         name="turn",
-        grid=(GROUPS,),
+        grid=(CHIPS,),
         out_shape=jax.ShapeDtypeStruct((ROWS, DEPTH), BF16),
-        in_specs=[pl.BlockSpec((BRICK, HEADS, LANE), lambda i: (i, 0, 0))],
-        out_specs=pl.BlockSpec((ROWS, BRICK), lambda i: (0, i)),
+        in_specs=[pl.BlockSpec((ROWS, HEADS, LANE), lambda i: (i, 0, 0))],
+        out_specs=pl.BlockSpec((ROWS, ROWS), lambda i: (0, i)),
         compiler_params=pltpu.CompilerParams(vmem_limit_bytes=VMEM_CAP),
         cost_estimate=cost(1),
     )(w)

time: 581 us -> 579 us (level)
  no operation moved by 1% of the time
where the time goes in v4:
time: 579 us; the launch traced here: 578 us
  Pallas kernels  547 us (94%)
  starting transfers between devices  11.9 us (2%)
  other arithmetic  9.11 us (2%)
  waiting for transfers between devices  8.57 us (1%)
    pallas_call x1, Pallas kernels, exchange(): pl.pallas_call(exchange_kernel, name='exchange', out_shape=[jax.ShapeDtyp...  433 us
    pallas_call x1, Pallas kernels, attention(): pl.pallas_call(functools.partial(attn_kernel, q_scale), name='attention',...  37.5 us
    pallas_call x1, Pallas kernels, finish(): pl.pallas_call(finish_kernel, name='finish', grid=(steps,), out_shape=[ja...  34.6 us
    pallas_call x1, Pallas kernels, projections(): pl.pallas_call(functools.partial(proj_kernel, q_scale), name='projections...  34.5 us
  transfers between devices with their start and end apart: 3, of which 1 were waited for; matrix products, arithmetic and copies ran while one was open for 1% of the time, Pallas kernels for 12%

profile of v4, /device:TPU:0, one launch (start us, length us, event | category | flops | bytes accessed | tf_op | source)
XLA Modules:
  0.0 577.7 jit_solution(13537288781599715761)
XLA Ops:
  0.6 8.0 %turn.1.wq_ref.refs_3_ = bf16[1024,4096]{1,0:T(8,128)(2,1)} custom-call(bf16[4096,8,128]{2,1,0:T(8,128)(2,1)} %w_ref.1), custom_call_target="tpu_custom_call" | custom-call | flops 1000000000 | bytes 100000000 | tf_op jit(solution)/shard_map/turn/pallas_call | solution.py:157
  8.6 5.6 broadcast_select_fusion
  14.2 7.3 %collective-permute-start.2 = (bf16[512,2048]{1,0:T(8,128)(2,1)}, bf16[512,2048]{1,0:T(8,128)(2,1)}, u32[]{:S(2)}, u32[]{:S(2)}) collective-permute-start(bf16[512,2048]{1,0:T(8,128)(2,1)} %get-tuple-element.40), channel_id=1, source_target_pairs={{24,8},{0,16},{25,9},{1,17},{26,10},{2,18},{27,11},{3,19},{28,12},... | collective-permute-start | bytes 6291464 | tf_op jit(solution)/shard_map/ppermute | solution.py:833
  21.5 2.0 collective-permute-start.1
  23.5 2.6 collective-permute-start
  26.1 0.2 multiply_cosine_fusion.1
  26.3 0.3 fusion.1
  26.6 0.7 pad_maximum_fusion.cos_ref
  27.3 0.9 fusion.mask_ref
  28.2 0.6 pad_maximum_fusion.2.refs_12_
  28.9 0.7 pad_maximum_fusion.1.sin_ref
  29.6 34.5 %projections.1 = (bf16[1024,1024]{1,0:T(8,128)(2,1)}, bf16[1024,1024]{1,0:T(8,128)(2,1)}, bf16[8,1024,256]{2,1,0:T(8,128)(2,1)}) custom-call(bf16[1024,4096]{1,0:T(8,128)(2,1)} %bitcast.11, bf16[1024,4096]{1,0:T(8,128)(2,1)} %bitcast.13, bf16[1024,4096]{1,0:T(8,128)(2,1)} %turn.1.wq_ref.refs_3_, bf16[1024,4096]{1,0:T(8,128)(2,1)} %bitcast.8, ...), custom_call_target="tpu_custom_call" | custom-call | flops 20000000000 | bytes 100000000 | tf_op jit(solution)/shard_map/projections/pallas_call | solution.py:172
  64.1 37.5 %attention.1 = (bf16[1024,1024]{1,0:T(8,128)(2,1)}, bf16[1024,1024]{1,0:T(8,128)(2,1)}, f32[8,2,256,512]{3,2,1,0:T(8,128)}) custom-call(bf16[1024,1024]{1,0:T(8,128)(2,1)} %get-tuple-element.23.q_ref, bf16[1024,1024]{1,0:T(8,128)(2,1)} %get-tuple-element.24.do_ref, bf16[8,1024,256]{2,1,0:T(8,128)(2,1)} %get-tuple-element.25.kv_ref, ...), custom_call_target="tpu_custom_call" | custom-call | flops 30000001024 | bytes 100000000 | tf_op jit(solution)/shard_map/attention/pallas_call | solution.py:216
  101.6 8.6 %collective-permute-done.refs_4_ = bf16[512,2048]{1,0:T(8,128)(2,1)} collective-permute-done((bf16[512,2048]{1,0:T(8,128)(2,1)}, bf16[512,2048]{1,0:T(8,128)(2,1)}, u32[]{:S(2)}, u32[]{:S(2)}) %collective-permute-start) | collective-permute-done | bytes 2097184 | tf_op jit(solution)/shard_map/ppermute | solution.py:831
  110.1 0.0 collective-permute-done.2.refs_6_
  110.1 0.0 collective-permute-done.1.refs_5_
  110.2 432.9 %exchange.1 = (bf16[1024,4096]{1,0:T(8,128)(2,1)}, bf16[1024,4096]{1,0:T(8,128)(2,1)}, f32[1024,4096]{1,0:T(8,128)}, f32[4096,1024]{1,0:T(8,128)}, f32[4096,256]...) custom-call(bf16[1024,1024]{1,0:T(8,128)(2,1)} %get-tuple-element.26, ...), custom_call_target="tpu_custom_call" | custom-call | flops 299999985664 | bytes 100000000 | tf_op jit(solution)/shard_map/exchange/pallas_call | solution.py:784
  543.1 34.6 %finish.1 = (bf16[1024,4096]{1,0:T(8,128)(2,1)}, bf16[1024,4096]{1,0:T(8,128)(2,1)}, f32[1024,4096]{1,0:T(8,128)}, f32[4096,8,128]{2,1,0:T(8,128)}, f32[4096,128]{1,0:T(8,128)}, /*index=5*/f32[4096,128]{1,0:T(8,128)}) custom-call(bf16[1024,4096]{1,0:T(8,128)(2,1)} %get-tuple-element.29.out_ref, bf16[1024,4096]{1,0:T(8,128)(2,1)} %get-tuple-element.30.dh_ref, ...), custom_call_target="tpu_custom_call" | custom-call | flops 1000000000 | bytes 100000000 | tf_op jit(solution)/shard_map/finish/pallas_call | solution.py:809
  (2 shorter events, 0.0 us)
Async XLA Ops:
  14.2 96.0 %collective-permute-start.2 = (bf16[512,2048]{1,0:T(8,128)(2,1)}, bf16[512,2048]{1,0:T(8,128)(2,1)}, u32[]{:S(2)}, u32[]{:S(2)}) collective-permute-start(bf16[512,2048]{1,0:T(8,128)(2,1)} %get-tuple-element.40), channel_id=1, source_target_pairs={{24,8},{0,16},{25,9},{1,17},{26,10},{2,18},{27,11},{3,19},{28,12},... | collective-permute-start | bytes 6291464 | tf_op jit(solution)/shard_map/ppermute | solution.py:833
  21.5 88.7 %collective-permute-start.1 = (bf16[512,2048]{1,0:T(8,128)(2,1)}, bf16[512,2048]{1,0:T(8,128)(2,1)}, u32[]{:S(2)}, u32[]{:S(2)}) collective-permute-start(bf16[512,2048]{1,0:T(8,128)(2,1)} %get-tuple-element.40), channel_id=1, source_target_pairs={{16,8},{8,16},{17,9},{9,17},{18,10},{10,18},{19,11},{11,19},{20,12... | collective-permute-start | bytes 6291464 | tf_op jit(solution)/shard_map/ppermute | solution.py:832
  23.5 86.7 %collective-permute-start = (bf16[512,2048]{1,0:T(8,128)(2,1)}, bf16[512,2048]{1,0:T(8,128)(2,1)}, u32[]{:S(2)}, u32[]{:S(2)}) collective-permute-start(bf16[512,2048]{1,0:T(8,128)(2,1)} %get-tuple-element.41), channel_id=1, source_target_pairs={{0,8},{24,16},{1,9},{25,17},{2,10},{26,18},{3,11},{27,19},{4,12},{... | collective-permute-start | bytes 6291464 | tf_op jit(solution)/shard_map/ppermute | solution.py:831
